TPU v7x, 32 devices: a whole 2x2x4 slice. The times are simulated.
32 devices in a mesh: px: 4 (over y, x), py: 8 (over z, core).
Axes of the slice: x: 2, y: 2, z: 4, core: 2. Of those that a mesh axis runs over, the one named last changes fastest.
Arguments:
- velocity: float32 [3, 8, 256, 1024], P(None, None, 'py', 'px'), may hold values from -6 to 6
- thickness: float32 [8, 256, 1024], P(None, 'py', 'px'), may hold values from 1 to 4
- velocity_tendency: float32 [3, 8, 256, 1024], P(None, None, 'py', 'px'), may hold values from -6 to 6
- thickness_tendency: float32 [8, 256, 1024], P(None, 'py', 'px'), may hold values from -0.5 to 0.5
- cell_distance: float32 [3, 256, 1024], P(None, 'py', 'px'), may hold values from 0.5 to 2
- edge_length: float32 [3, 256, 1024], P(None, 'py', 'px'), may hold values from 0.5 to 2
- cell_area: float32 [256, 1024], P('py', 'px'), may hold values from 1 to 4
- kite_area: float32 [2, 3, 256, 1024], P(None, None, 'py', 'px'), may hold values from 0.2 to 0.8
- coriolis: float32 [2, 256, 1024], P(None, 'py', 'px'), may hold values from -1 to 1
Outputs:
- vertex_potential: float32 [2, 8, 256, 1024], P(None, None, 'py', 'px')
- kinetic_energy: float32 [8, 256, 1024], P(None, 'py', 'px')
- cell_potential: float32 [8, 256, 1024], P(None, 'py', 'px')
- edge_potential: float32 [3, 8, 256, 1024], P(None, None, 'py', 'px')
All inputs are finite; a program needn't handle non-finite values.
Results may differ from a plain program's by a relative error of at most 0.00002.
Values sent between devices are 32-bit elements; how exact they have to be, the bound alone decides.
A program may use at most 64 MiB of HBM per device.

v0:
```python
import jax
import jax.numpy as jnp
from jax import lax
from jax.experimental import pallas as pl
from jax.experimental.pallas import tpu as pltpu
from jax.sharding import PartitionSpec as P

SUB = 8
LANE = 128
COMPS = 8
GEO = 14
DEPTH = 2
LANE_STEP = 2 * COMPS
MESH = pl.DeviceIdType.MESH


def iotas():
    sub = lax.broadcasted_iota(jnp.int32, (SUB, LANE), 0)
    lane = lax.broadcasted_iota(jnp.int32, (SUB, LANE), 1)
    return sub, lane


def exchange_kernel(counts, *refs):
    (vel, th, vt, tt, cd, el, kite, cor) = refs[:8]
    (o_bot, o_top, o_right, o_left, o_br, o_tr, o_bl) = refs[8:15]
    bufs = refs[15:23]
    (p_bot, p_top, p_right, p_left) = refs[23:27]
    in_sem, send_sem, recv_sem = refs[27:30]
    ny, nx = counts
    py, px = lax.axis_index("py"), lax.axis_index("px")
    down, up = lax.rem(py + 1, ny), lax.rem(py + ny - 1, ny)
    right, left = lax.rem(px + 1, nx), lax.rem(px + nx - 1, nx)

    loads = [
        pltpu.make_async_copy(src, dst, in_sem.at[i])
        for i, (src, dst) in enumerate(zip((vel, th, vt, tt, cd, el, kite, cor), bufs))
    ]
    for i in (4, 5, 6, 7, 0, 1, 2, 3):
        loads[i].start()
    barrier = pltpu.get_barrier_semaphore()
    near = [
        (up, px), (down, px), (py, left), (py, right),
        (up, left), (up, right), (down, left), (down, right),
    ]
    for y, x in near:
        pl.semaphore_signal(barrier, inc=1, device_id={"py": y, "px": x}, device_id_type=MESH)

    b_vel, b_th, b_vt, b_tt, b_cd, b_el, b_kite, b_cor = bufs
    levels, rows, cols = b_th.shape
    nr, nc = rows // SUB, cols // LANE
    sub, lane = iotas()
    last = slice(cols - LANE, cols)

    def view(ref, *lead):
        return lambda r, c: ref[lead + (r, c)]

    def level_comps(l):
        return (
            [view(b_vel, k, l) for k in range(3)]
            + [view(b_th, l)]
            + [view(b_vt, k, l) for k in range(3)]
            + [view(b_tt, l)]
        )

    geo = (
        [view(b_cd, k) for k in range(3)]
        + [view(b_el, k) for k in range(3)]
        + [view(b_kite, v, k) for v in range(2) for k in range(3)]
        + [view(b_cor, v) for v in range(2)]
    )

    def pack_rows(comps, base):
        for g in range(0, len(comps), 4):
            for c in range(nc):
                cs = slice(c * LANE, (c + 1) * LANE)
                bot = top = jnp.zeros((SUB, LANE), jnp.float32)
                for q, f in enumerate(comps[g : g + 4]):
                    m = jnp.where(sub < 4, f(slice(0, SUB), cs), f(slice(rows - SUB, rows), cs))
                    m = pltpu.roll(m, 2 * q, 0) if q else m
                    bot = jnp.where((sub == 2 * q) | (sub == 2 * q + 1), m, bot)
                    t = (2 * q + 6) % SUB
                    top = jnp.where((sub == t) | (sub == t + 1), m, top)
                at = slice(base + 2 * g, base + 2 * g + SUB)
                p_bot[at, cs] = bot
                p_top[at, cs] = top

    def pack_cols(items, tile):
        for r in range(nr):
            rs = slice(r * SUB, (r + 1) * SUB)
            ra = la = jnp.zeros((SUB, LANE), jnp.float32)
            for s, f in items:
                m = jnp.where(lane < LANE // 2, f(rs, slice(0, LANE)), f(rs, last))
                m = pltpu.roll(m, s, 1) if s else m
                ra = jnp.where((lane == s) | (lane == s + 1), m, ra)
                la = jnp.where(lane == (s + LANE - 1) % LANE, m, la)
            cs = slice(tile * LANE, (tile + 1) * LANE)
            p_right[rs, cs] = ra
            p_left[rs, cs] = la

    plan = [
        (p_bot, o_bot, (up, px)),
        (p_top, o_top, (down, px)),
        (p_right.at[rows - SUB : rows], o_tr, (down, left)),
        (p_right.at[0:SUB], o_br, (up, left)),
        (p_left.at[0:SUB], o_bl, (up, right)),
        (p_right, o_right, (py, left)),
        (p_left, o_left, (py, right)),
    ]
    copies = [
        pltpu.make_async_remote_copy(
            src_ref=src,
            dst_ref=dst,
            send_sem=send_sem.at[i],
            recv_sem=recv_sem.at[i],
            device_id={"py": y, "px": x},
            device_id_type=MESH,
        )
        for i, (src, dst, (y, x)) in enumerate(plan)
    ]
    for i in (4, 5, 6, 7):
        loads[i].wait()
    pack_rows(geo, levels * LANE_STEP)
    pack_cols([(2 * k, f) for k, f in enumerate(geo)], 1)
    for i in (0, 1, 2, 3):
        loads[i].wait()
    for l in range(levels):
        pack_rows(level_comps(l), l * LANE_STEP)
    pl.semaphore_wait(barrier, len(near))
    for copy in copies[:2]:
        copy.start()
    items = []
    for l in range(levels):
        comps = level_comps(l)
        items += [(l * LANE_STEP + 2 * k, f) for k, f in enumerate(comps)]
    pack_cols(items, 0)
    for copy in copies[2:]:
        copy.start()
    for copy in copies:
        copy.wait()


def exchange(counts, vel, th, vt, tt, cd, el, kite, cor):
    levels, rows, cols = th.shape
    f32 = jnp.float32
    band = (levels * LANE_STEP + 32, cols)
    side = (rows, 2 * LANE)
    corner = (SUB, 2 * LANE)
    args = (vel, th, vt, tt, cd, el, kite, cor)
    outs = (band, band, side, side, corner, corner, corner)
    return pl.pallas_call(
        lambda *refs: exchange_kernel(counts, *refs),
        out_shape=[jax.ShapeDtypeStruct(s, f32) for s in outs],
        in_specs=[pl.BlockSpec(memory_space=pl.ANY)] * len(args),
        out_specs=[pl.BlockSpec(memory_space=pl.ANY)] * len(outs),
        scratch_shapes=[pltpu.VMEM(a.shape, f32) for a in args]
        + [pltpu.VMEM(s, f32) for s in (band, band, side, side)]
        + [
            pltpu.SemaphoreType.DMA((len(args),)),
            pltpu.SemaphoreType.DMA((len(outs),)),
            pltpu.SemaphoreType.DMA((len(outs),)),
        ],
        compiler_params=pltpu.CompilerParams(collective_id=0, has_side_effects=True),
        name="exchange",
    )(*args)


class Field:
    def __init__(self, grid, make):
        self.grid, self.make, self.memo = grid, make, {}

    def __call__(self, r, c):
        key = (r % self.grid[0], c % self.grid[1])
        if key not in self.memo:
            self.memo[key] = self.make(*key)
        return self.memo[key]


def step_kernel(
    vel, th, vt, tt, cd, el, kite, cor, area,
    bot, top, gbot, gtop, right, left, br, tr, bl,
    o_vert, o_kin, o_cell, o_edge, geo, scale,
):
    level = pl.program_id(0)
    rows, cols = area.shape
    nr, nc = rows // SUB, cols // LANE
    grid = (nr + 1, nc + 1)
    sub, lane = iotas()

    def at(r, c):
        return (slice(r * SUB, (r + 1) * SUB), slice(c * LANE, (c + 1) * LANE))

    def lift(fn, *fields):
        return Field(grid, lambda r, c: fn(*[f(r, c) for f in fields]))

    def row_shift(f, a):
        rolled = Field(grid, lambda r, c: pltpu.roll(f(r, c), (-a) % SUB, 0))
        if a == 1:
            return Field(grid, lambda r, c: jnp.where(sub < SUB - 1, rolled(r, c), rolled(r + 1, c)))
        return Field(grid, lambda r, c: jnp.where(sub > 0, rolled(r, c), rolled(r - 1, c)))

    def col_shift(f, b):
        rolled = Field(grid, lambda r, c: pltpu.roll(f(r, c), (-b) % LANE, 1))
        if b == 1:
            return Field(grid, lambda r, c: jnp.where(lane < LANE - 1, rolled(r, c), rolled(r, c + 1)))
        return Field(grid, lambda r, c: jnp.where(lane > 0, rolled(r, c), rolled(r, c - 1)))

    def extended(own, k, band_bot, band_top, side):
        q, g = k % 4, k // 4

        def make(r, c):
            if c < nc:
                b, t = band_bot[at(g, c)], band_top[at(g, c)]
                m = jnp.where((sub == 2 * q) | (sub == 2 * q + 1), b, t)
                return pltpu.roll(m, (-2 * q) % SUB, 0) if q else m
            rt, lt = side(r)
            m = jnp.where((lane == 2 * k) | (lane == 2 * k + 1), rt, lt)
            return pltpu.roll(m, (-2 * k) % LANE, 1) if k else m

        halo = Field(grid, make)

        def tile(r, c):
            r, c = r % grid[0], c % grid[1]
            return own(*at(r, c)) if r < nr and c < nc else halo(r, c)

        return tile

    def side_of(tile, turn):
        cs = slice(tile * LANE, (tile + 1) * LANE)
        memo = {}

        def side(r):
            if r not in memo:
                if r < nr:
                    rs = slice(r * SUB, (r + 1) * SUB)
                    pair = right[rs, cs], left[rs, cs]
                else:
                    pair = jnp.where(sub < 4, br[:, cs], tr[:, cs]), bl[:, cs]
                memo[r] = tuple(turn(x) for x in pair)
            return memo[r]

        return side

    def view(ref, *lead):
        return lambda r, c: ref[lead + (r, c)]

    @pl.when(level == 0)
    def _():
        side = side_of(1, lambda x: x)
        owns = (
            [view(cd, k) for k in range(3)]
            + [view(el, k) for k in range(3)]
            + [view(kite, v, k) for v in range(2) for k in range(3)]
            + [view(cor, v) for v in range(2)]
        )
        f = [extended(own, k, gbot, gtop, side) for k, own in enumerate(owns)]
        for r in range(nr + 1):
            for c in range(nc + 1):
                for k in range(3):
                    geo[(k,) + at(r, c)] = f[k](r, c)
                    geo[(3 + k,) + at(r, c)] = 0.25 * f[k](r, c) * f[3 + k](r, c)
                for k in range(6):
                    geo[(6 + k,) + at(r, c)] = f[6 + k](r, c)
                for v in range(2):
                    t = f[6 + 3 * v](r, c) + f[7 + 3 * v](r, c) + f[8 + 3 * v](r, c)
                    geo[(12 + v,) + at(r, c)] = f[12 + v](r, c) * t
                if r < nr and c < nc:
                    for k in range(3):
                        scale[(k,) + at(r, c)] = (-0.5 / 36.0) / f[k](r, c)
                    scale[(3,) + at(r, c)] = 1.0 / area[at(r, c)]

    turn_by = lax.rem(LANE - level * (DEPTH * LANE_STEP), LANE)
    side = side_of(0, lambda x: pltpu.roll(x, turn_by, 1))
    for u in range(DEPTH):
        owns = (
            [view(vel, k, u) for k in range(3)]
            + [view(th, u)]
            + [view(vt, k, u) for k in range(3)]
            + [view(tt, u)]
        )
        x = [extended(own, u * COMPS + k, bot, top, side) for k, own in enumerate(owns)]
        v, h, t, g = x[0:3], x[3], x[4:7], x[7]

        def geo_tile(k):
            return lambda r, c: geo[(k,) + at(r % grid[0], c % grid[1])]

        dist = [geo_tile(k) for k in range(3)]
        ew = [geo_tile(3 + k) for k in range(3)]
        kt = [geo_tile(6 + k) for k in range(6)]
        ct = [geo_tile(12 + k) for k in range(2)]

        def parts(vv, hh):
            flux = [lift(lambda a, b: a * b, vv[k], dist[k]) for k in range(3)]
            c0 = lift(lambda a, b, c: a + b - c, flux[0], row_shift(flux[2], 1), flux[1])
            c1 = lift(
                lambda a, b, c: a - b - c, flux[1], flux[2], col_shift(row_shift(flux[0], -1), 1)
            )
            hc = col_shift(hh, 1)
            hr = row_shift(hh, 1)
            hd = row_shift(hc, -1)
            mix = lambda a, b, c, p, q, s: a * p + b * q + c * s
            h0 = lift(mix, kt[0], kt[1], kt[2], hh, hr, hc)
            h1 = lift(mix, kt[3], kt[4], kt[5], hh, hc, hd)
            return (c0, c1), (h0, h1)

        cv, hv = parts(v, h)
        cw, hw = parts(t, g)

        def potential(k):
            def make(r, c):
                a0 = ct[k](r, c) + cv[k](r, c)
                a1 = cw[k](r, c)
                b0 = hv[k](r, c)
                b1 = hw[k](r, c)
                bm, be = b0 + 0.5 * b1, b0 + b1
                m = bm * be
                scale_all = 1.0 / (b0 * m)
                mid = (a0 + a0 + a1) * (b0 * be)
                late = mid + (a0 + a1) * (b0 * bm)
                return (a0 * m + mid + late) * scale_all, late * scale_all

            both = Field(grid, make)
            return Field(grid, lambda r, c: both(r, c)[0]), Field(grid, lambda r, c: both(r, c)[1])

        p0, q0 = potential(0)
        p1, q1 = potential(1)
        add = lambda a, b: a + b
        add3 = lambda a, b, c: a + b + c

        def cell(f0, f1):
            f0_up = row_shift(f0, -1)
            f1_down = row_shift(f1, 1)
            pair = lift(add, f0, f1)
            return lift(add3, pair, f0_up, col_shift(lift(add, pair, f1_down), -1)), f0_up, f1_down, pair

        cc, p0_up, p1_down, pair = cell(p0, p1)
        dd = cell(q0, q1)[0]
        p1_low = col_shift(p1_down, -1)

        def neighbours(f):
            fc = col_shift(f, 1)
            return row_shift(f, 1), fc, row_shift(fc, -1)

        cn, dn = neighbours(cc), neighbours(dd)
        ends = [lift(add, p0, p1_low), pair, lift(add, p1, p0_up)]
        en = [
            lift(lambda w, a, b: w * (a * (a + b) + (1.0 / 3.0) * (b * b)), ew[k], v[k], t[k])
            for k in range(3)
        ]
        e_up = row_shift(en[0], -1)
        e_low = col_shift(lift(add, en[1], row_shift(en[2], 1)), -1)

        for r in range(nr):
            for c in range(nc):
                p = at(r, c)
                o_vert[(0, u) + p] = p0(r, c) * (1.0 / 6.0)
                o_vert[(1, u) + p] = p1(r, c) * (1.0 / 6.0)
                total = en[0](r, c) + en[1](r, c) + en[2](r, c) + e_up(r, c) + e_low(r, c)
                o_kin[(u,) + p] = total * scale[(3,) + p]
                o_cell[(u,) + p] = cc(r, c) * (1.0 / 36.0)
                for k in range(3):
                    slope = v[k](r, c) * (cn[k](r, c) - cc(r, c)) + t[k](r, c) * (dn[k](r, c) - dd(r, c))
                    o_edge[(k, u) + p] = ends[k](r, c) * (1.0 / 12.0) + scale[(k,) + p] * slope


def local(counts, vel, th, vt, tt, cd, el, area, kite, cor):
    bot, top, right, left, br, tr, bl = exchange(counts, vel, th, vt, tt, cd, el, kite, cor)
    levels, rows, cols = th.shape
    f32 = jnp.float32
    whole = lambda a: pl.BlockSpec(a.shape, lambda l: (0,) * a.ndim)
    three = pl.BlockSpec((3, DEPTH, rows, cols), lambda l: (0, l, 0, 0))
    two = pl.BlockSpec((2, DEPTH, rows, cols), lambda l: (0, l, 0, 0))
    one = pl.BlockSpec((DEPTH, rows, cols), lambda l: (l, 0, 0))
    band = pl.BlockSpec((DEPTH * LANE_STEP, cols), lambda l: (l, 0))
    gband = pl.BlockSpec((32, cols), lambda l: (levels * LANE_STEP // 32, 0))
    return pl.pallas_call(
        step_kernel,
        grid=(levels // DEPTH,),
        out_shape=[
            jax.ShapeDtypeStruct((2, levels, rows, cols), f32),
            jax.ShapeDtypeStruct((levels, rows, cols), f32),
            jax.ShapeDtypeStruct((levels, rows, cols), f32),
            jax.ShapeDtypeStruct((3, levels, rows, cols), f32),
        ],
        in_specs=[
            three, one, three, one, whole(cd), whole(el), whole(kite), whole(cor), whole(area),
            band, band, gband, gband, whole(right), whole(left), whole(br), whole(tr), whole(bl),
        ],
        out_specs=[two, one, one, three],
        scratch_shapes=[
            pltpu.VMEM((GEO, rows + SUB, cols + LANE), f32),
            pltpu.VMEM((4, rows, cols), f32),
        ],
        name="step",
    )(vel, th, vt, tt, cd, el, kite, cor, area, bot, top, bot, top, right, left, br, tr, bl)


def solution(mesh):
    counts = (mesh.shape["py"], mesh.shape["px"])
    p4, p3 = P(None, None, "py", "px"), P(None, "py", "px")
    return jax.shard_map(
        lambda *args: local(counts, *args),
        mesh=mesh,
        in_specs=(p4, p3, p4, p3, p3, p3, P("py", "px"), p4, p3),
        out_specs=(p4, p3, p3, p4),
        check_vma=False,
    )
```

profile of v0, /device:TPU:0, one launch (start us, length us, event | category | flops | bytes accessed | tf_op | source)
XLA Modules:
  0.0 19.8 jit_solution(14418759220974245245)
XLA Ops:
  0.6 11.9 %exchange.1 = (f32[160,256]{1,0:T(8,128)}, f32[160,256]{1,0:T(8,128)}, f32[32,256]{1,0:T(8,128)}, f32[32,256]{1,0:T(8,128)}, f32[8,256]{1,0:T(8,128)}, /*index=5*/f32[8,256]{1,0:T(8,128)}, f32[8,256]{1,0:T(8,128)}) custom-call(f32[3,8,32,256]{3,2,1,0:T(8,128)} %vel.1, f32[8,32,256]{2,1,0:T(8,128)} %th.1, f32[3,8,32,256]{3,2,1,0:T(8,128)} %vt.1, ...), custom_call_target="tpu_custom_call" | custom-call | tf_op jit(solution)/shard_map/exchange/pallas_call | solution.py:150
  12.5 7.3 %step.1 = (f32[2,8,32,256]{3,2,1,0:T(8,128)}, f32[8,32,256]{2,1,0:T(8,128)}, f32[8,32,256]{2,1,0:T(8,128)}, f32[3,8,32,256]{3,2,1,0:T(8,128)}) custom-call(f32[3,8,32,256]{3,2,1,0:T(8,128)} %vel.1, f32[8,32,256]{2,1,0:T(8,128)} %th.1, f32[3,8,32,256]{3,2,1,0:T(8,128)} %vt.1, f32[8,32,256]{2,1,0:T(8,128)} %tt.1, f32[3,32,256]{2,1,0:T(8,128)} %cd.1, ...), custom_call_target="tpu_custom_call" | custom-call | tf_op jit(solution)/shard_map/step/pallas_call | solution.py:375
where the time goes:
time: 20 us; the launch traced here: 19.8 us
  Pallas kernels  19.2 us (96%)
  between operations  0.64 us (3%)
    pallas_call x1, Pallas kernels, exchange(): pl.pallas_call(lambda *refs: exchange_kernel(counts, *refs), out_shape=[j...  11.9 us
    pallas_call x1, Pallas kernels, local(): pl.pallas_call(step_kernel, grid=(levels // DEPTH,), out_shape=[jax.Shape...  7.33 us

commit v1 on v0

v1 whole, which is shorter than its diff:
```python
import jax
import jax.numpy as jnp
from jax import lax
from jax.experimental import pallas as pl
from jax.experimental.pallas import tpu as pltpu
from jax.sharding import PartitionSpec as P

SUB = 8
LANE = 128
GROUP = 16
PAIR = 2
MESH = pl.DeviceIdType.MESH
F32 = jnp.float32
SLOPE = -0.5 / 36.0


def iotas():
    sub = lax.broadcasted_iota(jnp.int32, (SUB, LANE), 0)
    lane = lax.broadcasted_iota(jnp.int32, (SUB, LANE), 1)
    return sub, lane


def roll(x, shift, axis):
    n = (SUB, LANE)[axis]
    return pltpu.roll(x, shift % n, axis) if shift % n else x


def span(r, c):
    return (slice(r * SUB, (r + 1) * SUB), slice(c * LANE, (c + 1) * LANE))


class Field:
    def __init__(self, grid, make):
        self.grid, self.make, self.memo = grid, make, {}

    def __call__(self, r, c):
        key = (r % self.grid[0], c % self.grid[1])
        if key not in self.memo:
            self.memo[key] = self.make(*key)
        return self.memo[key]


def chain(grid, v, h, t, g, dist, ew, kt, ct, swap=lambda i, f: f):
    sub, lane = iotas()

    def lift(fn, *fields):
        return Field(grid, lambda r, c: fn(*[f(r, c) for f in fields]))

    def row_shift(f, a):
        rolled = Field(grid, lambda r, c: roll(f(r, c), -a, 0))
        if grid[0] == 1:
            return rolled
        keep = sub < SUB - 1 if a == 1 else sub > 0
        return Field(grid, lambda r, c: jnp.where(keep, rolled(r, c), rolled(r + a, c)))

    def col_shift(f, b):
        rolled = Field(grid, lambda r, c: roll(f(r, c), -b, 1))
        if grid[1] == 1:
            return rolled
        keep = lane < LANE - 1 if b == 1 else lane > 0
        return Field(grid, lambda r, c: jnp.where(keep, rolled(r, c), rolled(r, c + b)))

    def parts(vv, hh):
        flux = [lift(lambda a, b: a * b, vv[k], dist[k]) for k in range(3)]
        c0 = lift(lambda a, b, c: a + b - c, flux[0], row_shift(flux[2], 1), flux[1])
        c1 = lift(lambda a, b, c: a - b - c, flux[1], flux[2], col_shift(row_shift(flux[0], -1), 1))
        hc = col_shift(hh, 1)
        hr = row_shift(hh, 1)
        hd = row_shift(hc, -1)
        mix = lambda a, b, c, p, q, s: a * p + b * q + c * s
        h0 = lift(mix, kt[0], kt[1], kt[2], hh, hr, hc)
        h1 = lift(mix, kt[3], kt[4], kt[5], hh, hc, hd)
        return (c0, c1), (h0, h1)

    cv, hv = parts(v, h)
    cw, hw = parts(t, g)

    def potential(k):
        def make(r, c):
            a0 = ct[k](r, c) + cv[k](r, c)
            a1 = cw[k](r, c)
            b0 = hv[k](r, c)
            b1 = hw[k](r, c)
            bm, be = b0 + 0.5 * b1, b0 + b1
            m = bm * be
            scale_all = 1.0 / (b0 * m)
            mid = (a0 + a0 + a1) * (b0 * be)
            late = mid + (a0 + a1) * (b0 * bm)
            return (a0 * m + mid + late) * scale_all, late * scale_all

        both = Field(grid, make)
        return Field(grid, lambda r, c: both(r, c)[0]), Field(grid, lambda r, c: both(r, c)[1])

    p0, q0 = potential(0)
    p1, q1 = potential(1)
    add = lambda a, b: a + b
    add3 = lambda a, b, c: a + b + c

    def cell(f0, f1):
        f0_up = row_shift(f0, -1)
        f1_down = row_shift(f1, 1)
        pair = lift(add, f0, f1)
        return lift(add3, pair, f0_up, col_shift(lift(add, pair, f1_down), -1)), f0_up, f1_down, pair

    cc, p0_up, p1_down, pair = cell(p0, p1)
    dd = cell(q0, q1)[0]
    cc, dd = swap(0, cc), swap(1, dd)
    p1_low = col_shift(p1_down, -1)

    def neighbours(f):
        fc = col_shift(f, 1)
        return row_shift(f, 1), fc, row_shift(fc, -1)

    cn, dn = neighbours(cc), neighbours(dd)
    ends = [lift(add, p0, p1_low), pair, lift(add, p1, p0_up)]
    en = [
        lift(lambda w, a, b: w * (a * (a + b) + (1.0 / 3.0) * (b * b)), ew[k], v[k], t[k])
        for k in range(3)
    ]
    e_up = row_shift(en[0], -1)
    e_low = col_shift(lift(add, en[1], row_shift(en[2], 1)), -1)

    def outputs(scale):
        def edge(k):
            def make(r, c):
                slope = v[k](r, c) * (cn[k](r, c) - cc(r, c)) + t[k](r, c) * (dn[k](r, c) - dd(r, c))
                return ends[k](r, c) * (1.0 / 12.0) + scale[k](r, c) * slope

            return Field(grid, make)

        kin = Field(
            grid,
            lambda r, c: (en[0](r, c) + en[1](r, c) + en[2](r, c) + e_up(r, c) + e_low(r, c)) * scale[3](r, c),
        )
        return [
            lift(lambda a: a * (1.0 / 6.0), p0),
            lift(lambda a: a * (1.0 / 6.0), p1),
            kin,
            lift(lambda a: a * (1.0 / 36.0), cc),
        ] + [edge(k) for k in range(3)]

    return cc, dd, outputs


def main_kernel(counts, *refs):
    hbm = refs[:9]
    o_vert, o_kin, o_cell, o_edge = refs[9:13]
    bufs = refs[13:22]
    bands = refs[22:31]
    p_right, p_left, g_right, g_left = refs[31:35]
    geo, kgeo, sgeo, slev, saved = refs[35:40]
    in_sem, own_sem, send_row, recv_row, send_col, recv_col = refs[40:46]
    ny, nx = counts
    py, px = lax.axis_index("py"), lax.axis_index("px")
    down, up = lax.rem(py + 1, ny), lax.rem(py + ny - 1, ny)
    right, left = lax.rem(px + 1, nx), lax.rem(px + nx - 1, nx)

    barrier = pltpu.get_barrier_semaphore()
    near = [
        (up, px), (down, px), (py, left), (py, right),
        (up, left), (up, right), (down, left), (down, right),
    ]
    for y, x in near:
        pl.semaphore_signal(barrier, inc=1, device_id={"py": y, "px": x}, device_id_type=MESH)

    b_vel, b_th, b_vt, b_tt, b_cd, b_el, b_kite, b_cor, b_area = bufs
    levels, rows, cols = b_th.shape
    nr, nc = rows // SUB, cols // LANE
    sub, lane = iotas()
    pos, group = lane & (GROUP - 1), lane >> 4
    head, tail = slice(0, LANE), slice(cols - LANE, cols)

    loads = [pltpu.make_async_copy(a, b, in_sem.at[i]) for i, (a, b) in enumerate(zip(hbm, bufs))]
    for i in (4, 5, 6, 7, 0, 1, 2, 3, 8):
        loads[i].start()

    def part(ref, a, b):
        return ref.at[(slice(None),) * (len(ref.shape) - 2) + (slice(a, b), slice(None))]

    own = []
    for i, (a, b) in enumerate(zip(hbm, bands)):
        own.append(pltpu.make_async_copy(part(a, rows - 2, rows), part(b, 0, 2), own_sem.at[2 * i]))
        own.append(pltpu.make_async_copy(part(a, 0, 2), part(b, 6, 8), own_sem.at[2 * i + 1]))
    for copy in own:
        copy.start()

    def remote(src, dst, sems, i, y, x):
        return pltpu.make_async_remote_copy(
            src_ref=src,
            dst_ref=dst,
            send_sem=sems[0].at[i],
            recv_sem=sems[1].at[i],
            device_id={"py": y, "px": x},
            device_id_type=MESH,
        )

    row_copies = []
    for i, (a, b) in enumerate(zip(hbm[:8], bands)):
        sems = (send_row, recv_row)
        row_copies.append(remote(part(a, 0, 2), part(b, 2, 4), sems, 2 * i, up, px))
        row_copies.append(remote(part(a, rows - 2, rows), part(b, 4, 6), sems, 2 * i + 1, down, px))
    pl.semaphore_wait(barrier, len(near))
    for copy in row_copies:
        copy.start()

    def view(ref, *lead):
        return lambda r, c: ref[lead + (r, c)]

    def level_views(l, src):
        vel, th, vt, tt = src
        return (
            [view(vel, k, l) for k in range(3)]
            + [view(th, l)]
            + [view(vt, k, l) for k in range(3)]
            + [view(tt, l)]
        )

    def geo_views(src):
        cd, el, kite, cor = src
        return (
            [view(cd, k) for k in range(3)]
            + [view(el, k) for k in range(3)]
            + [view(kite, v, k) for v in range(2) for k in range(3)]
            + [view(cor, v) for v in range(2)]
        )

    def pack_cols(items, tile):
        for r in range(nr):
            rs = slice(r * SUB, (r + 1) * SUB)
            ra = la = jnp.zeros((SUB, LANE), F32)
            for s, f in items:
                m = jnp.where(lane < LANE // 2, f(rs, head), f(rs, tail))
                m = roll(m, s, 1)
                ra = jnp.where((lane == s) | (lane == s + 1), m, ra)
                la = jnp.where(lane == (s + LANE - 1) % LANE, m, la)
            cs = slice(tile * LANE, (tile + 1) * LANE)
            p_right[rs, cs] = ra
            p_left[rs, cs] = la

    for i in (4, 5, 6, 7):
        loads[i].wait()
    own_geo = geo_views(bufs[4:8])
    pack_cols([(2 * k, f) for k, f in enumerate(own_geo)], 1)
    for i in (0, 1, 2, 3):
        loads[i].wait()
    items = []
    for l in range(levels):
        items += [(l * GROUP + 2 * k, f) for k, f in enumerate(level_views(l, bufs[:4]))]
    pack_cols(items, 0)

    sems = (send_col, recv_col)
    col_copies = [
        remote(p_right, g_right.at[0:rows], sems, 0, py, left),
        remote(p_left, g_left.at[0:rows], sems, 1, py, right),
        remote(p_right.at[rows - 2 : rows], g_right.at[rows + 6 : rows + 8], sems, 2, down, left),
        remote(p_right.at[0:2], g_right.at[rows : rows + 2], sems, 3, up, left),
        remote(p_left.at[0:2], g_left.at[rows : rows + 2], sems, 4, up, right),
    ]
    for copy in col_copies:
        copy.start()
    loads[8].wait()

    def put_geo(dst, at, f, area=None):
        for k in range(3):
            dst[(k,) + at] = 0.25 * f[k] * f[3 + k]
            if area is not None:
                dst[(5 + k,) + at] = SLOPE / f[k]
        for v in range(2):
            dst[(3 + v,) + at] = f[12 + v] * (f[6 + 3 * v] + f[7 + 3 * v] + f[8 + 3 * v])
        if area is not None:
            dst[(8,) + at] = 1.0 / area

    for r in range(nr):
        for c in range(nc):
            put_geo(geo, span(r, c), [f(*span(r, c)) for f in own_geo], b_area[span(r, c)])

    def strip(fl, ft, l):
        m = jnp.where(lane < 5, fl, roll(ft, 9, 1))
        return roll(m, l * GROUP + 2, 1)

    def spread(x):
        for w in (GROUP, 2 * GROUP, 4 * GROUP):
            x = jnp.where(lane < w, x, roll(x, w, 1))
        return x

    def strip_levels(src, rs):
        out = []
        for k in range(8):
            acc = jnp.zeros((SUB, LANE), F32)
            for l in range(levels):
                f = level_views(l, src)[k]
                acc = jnp.where(group == l, strip(f(rs, head), f(rs, tail), l), acc)
            out.append(acc)
        return out

    for r in range(nr):
        rs = slice(r * SUB, (r + 1) * SUB)
        for k, x in enumerate(strip_levels(bufs[:4], rs)):
            slev[k, rs] = x
        for k, f in enumerate(own_geo):
            sgeo[k, rs] = strip(f(rs, head), f(rs, tail), 0)
        sgeo[14, rs] = spread(strip(b_area[rs, head], b_area[rs, tail], 0))

    def fields(grid, views):
        return [Field(grid, lambda r, c, f=f: f(*span(r, c))) for f in views]

    def run(grid, x, kites, dist, derived, swap=lambda i, f: f):
        f = fields(grid, derived)
        d = fields(grid, dist)
        cc, dd, outputs = chain(
            grid, x[0:3], x[3], x[4:7], x[7], d, f[0:3], fields(grid, kites), f[3:5], swap
        )
        return cc, dd, outputs(f[5:9])

    def block(l):
        grid = (nr, nc)
        cc, dd, outs = run(
            grid,
            fields(grid, level_views(l, bufs[:4])),
            own_geo[6:12],
            own_geo[0:3],
            [view(geo, k) for k in range(9)],
        )
        dst = [view_at(o_vert, 0, l), view_at(o_vert, 1, l), view_at(o_kin, l), view_at(o_cell, l)]
        dst += [view_at(o_edge, k, l) for k in range(3)]
        for c in range(nc):
            for i, f in enumerate((cc, dd)):
                saved[i, l, :, span(0, c)[1]] = jnp.where(
                    sub < 4, roll(f(nr - 1, c), 2, 0), roll(f(0, c), -2, 0)
                )
        for r in range(nr):
            for c in range(nc):
                for put, f in zip(dst, outs):
                    put(span(r, c), f(r, c))

    def view_at(ref, *lead):
        def put(at, x):
            ref[lead + at] = x

        return put

    def inner(i, carry):
        for u in range(PAIR):
            block(i * PAIR + u)
        return carry

    lax.fori_loop(0, levels // PAIR, inner, 0)

    for copy in own:
        copy.wait()
    for copy in row_copies + col_copies:
        copy.wait()

    band_geo = geo_views(bands[4:8])
    for c in range(nc):
        at = span(0, c)
        put_geo(kgeo, at, [f(*at) for f in band_geo], bands[8][at])

    merge = (sub == 0) | (sub == SUB - 1)
    for l in range(levels):
        grid = (1, nc)

        def swap(i, f, l=l):
            return Field(
                grid, lambda r, c: jnp.where(merge, saved[i, l, :, span(0, c)[1]], f(r, c))
            )

        outs = run(
            grid,
            fields(grid, level_views(l, bands[:4])),
            band_geo[6:12],
            band_geo[0:3],
            [view(kgeo, k) for k in range(9)],
            swap,
        )[2]
        dst = [(o_vert, (0, l)), (o_vert, (1, l)), (o_kin, (l,)), (o_cell, (l,))]
        dst += [(o_edge, (k, l)) for k in range(3)]
        both = ((rows - 1, 1, 1), (0, 6, 1))
        which = [
            ((rows - 1, 1, 1),),
            ((0, 6, 1),),
            both,
            both,
            ((rows - 2, 0, 2), (0, 6, 1)),
            both,
            ((rows - 1, 1, 1), (0, 6, 2)),
        ]
        for c in range(nc):
            cs = span(0, c)[1]
            for (ref, lead), f, ranges in zip(dst, outs, which):
                x = f(0, c)
                for to, src, n in ranges:
                    ref[lead + (slice(to, to + n), cs)] = x[src : src + n]

    def turn(x):
        return jnp.where(sub < 4, roll(x, -2, 0), roll(x, 2, 0))

    low = slice(0, SUB)
    edge_rows = slice(rows, rows + SUB)
    for k, x in enumerate(strip_levels(bands[:4], low)):
        slev[k, edge_rows] = turn(x)
    for k, f in enumerate(band_geo):
        sgeo[k, edge_rows] = turn(strip(f(low, head), f(low, tail), 0))

    def insert(x, k, rs, cs):
        rt = roll(g_right[rs, cs], 11 - 2 * k, 1)
        lt = roll(g_left[rs, cs], 2 - 2 * k, 1)
        return jnp.where((pos == 11) | (pos == 12), rt, jnp.where(pos == 1, lt, x))

    for r in range(nr + 1):
        rs = slice(r * SUB, (r + 1) * SUB)
        raw = [
            spread(insert(sgeo[k, rs], k, rs, slice(LANE, 2 * LANE))) for k in range(14)
        ]
        for k in list(range(3)) + list(range(6, 12)):
            sgeo[k, rs] = raw[k]
        ws = [0.25 * raw[k] * raw[3 + k] for k in range(3)]
        ts = [raw[12 + v] * (raw[6 + 3 * v] + raw[7 + 3 * v] + raw[8 + 3 * v]) for v in range(2)]
        for k, x in zip((3, 4, 5, 12, 13), ws + ts):
            sgeo[k, rs] = x

    grid = (nr + 1, 1)
    one = lambda r: slice(r * SUB, (r + 1) * SUB)
    sfield = lambda k: Field(grid, lambda r, c: sgeo[k, one(r)])
    x = [
        Field(grid, lambda r, c, k=k: insert(slev[k, one(r)], k, one(r), slice(0, LANE)))
        for k in range(8)
    ]
    outputs = chain(
        grid, x[0:3], x[3], x[4:7], x[7],
        [sfield(k) for k in range(3)],
        [sfield(k) for k in (3, 4, 5)],
        [sfield(k) for k in range(6, 12)],
        [sfield(k) for k in (12, 13)],
    )[2]
    scale = [Field(grid, lambda r, c, k=k: SLOPE / sgeo[k, one(r)]) for k in range(3)]
    scale.append(Field(grid, lambda r, c: 1.0 / sgeo[14, one(r)]))
    outs = outputs(scale)
    refs_of = [(o_vert, (0,)), (o_vert, (1,)), (o_kin, ()), (o_cell, ())]
    refs_of += [(o_edge, (k,)) for k in range(3)]
    first, ends = lane == 0, lane >= LANE - 2
    end = lane == LANE - 1
    masks = [(None, end), (None, end), (first, None), (first, end), (first, ends), (first, ends), (first, ends)]
    for r in range(nr):
        for (ref, lead), f, (mf, me) in zip(refs_of, outs, masks):
            y = f(r, 0)
            y = jnp.where(pos == 2, y, roll(y, -9, 1))
            for l in range(levels):
                z = roll(y, -(l * GROUP + 2), 1)
                if mf is not None:
                    pltpu.store(ref.at[lead + (l, one(r), head)], z, mask=mf)
                if me is not None:
                    pltpu.store(ref.at[lead + (l, one(r), tail)], z, mask=me)


def drain_kernel(*refs):
    src, dst, sem = refs[:4], refs[4:8], refs[8]
    copies = [pltpu.make_async_copy(a, b, sem.at[i]) for i, (a, b) in enumerate(zip(src, dst))]
    for copy in copies:
        copy.start()
    for copy in copies:
        copy.wait()


def local(counts, vel, th, vt, tt, cd, el, area, kite, cor):
    args = (vel, th, vt, tt, cd, el, kite, cor, area)
    levels, rows, cols = th.shape
    outs = [(2, levels, rows, cols), (levels, rows, cols), (levels, rows, cols), (3, levels, rows, cols)]
    band = lambda a: a.shape[:-2] + (SUB, cols)
    hbm, vmem = pl.BlockSpec(memory_space=pl.ANY), pl.BlockSpec(memory_space=pltpu.VMEM)
    side = (rows + SUB, 2 * LANE)
    kept = pl.pallas_call(
        lambda *refs: main_kernel(counts, *refs),
        out_shape=[pltpu.VMEM(s, F32) for s in outs],
        in_specs=[hbm] * len(args),
        out_specs=[vmem] * len(outs),
        scratch_shapes=[pltpu.VMEM(a.shape, F32) for a in args]
        + [pltpu.VMEM(band(a), F32) for a in args]
        + [pltpu.VMEM(s, F32) for s in ((rows, 2 * LANE), (rows, 2 * LANE), side, side)]
        + [
            pltpu.VMEM((9, rows, cols), F32),
            pltpu.VMEM((9, SUB, cols), F32),
            pltpu.VMEM((15, rows + SUB, LANE), F32),
            pltpu.VMEM((8, rows + SUB, LANE), F32),
            pltpu.VMEM((2, levels, SUB, cols), F32),
            pltpu.SemaphoreType.DMA((9,)),
            pltpu.SemaphoreType.DMA((18,)),
            pltpu.SemaphoreType.DMA((16,)),
            pltpu.SemaphoreType.DMA((16,)),
            pltpu.SemaphoreType.DMA((5,)),
            pltpu.SemaphoreType.DMA((5,)),
        ],
        compiler_params=pltpu.CompilerParams(collective_id=0, has_side_effects=True),
        name="main",
    )(*args)
    return pl.pallas_call(
        drain_kernel,
        out_shape=[jax.ShapeDtypeStruct(s, F32) for s in outs],
        in_specs=[vmem] * len(outs),
        out_specs=[hbm] * len(outs),
        scratch_shapes=[pltpu.SemaphoreType.DMA((len(outs),))],
        name="drain",
    )(*kept)


def solution(mesh):
    counts = (mesh.shape["py"], mesh.shape["px"])
    p4, p3 = P(None, None, "py", "px"), P(None, "py", "px")
    return jax.shard_map(
        lambda *args: local(counts, *args),
        mesh=mesh,
        in_specs=(p4, p3, p4, p3, p3, p3, P("py", "px"), p4, p3),
        out_specs=(p4, p3, p3, p4),
        check_vma=False,
    )
```

time: 20 us -> 37.8 us (1.89)
  Pallas kernels: 19.2 us -> 33.9 us
  local copies, waits for them, and re-layouts: 0 us -> 3.09 us
    pallas_call x2, Pallas kernels: 19.2 us -> 33.9 us  [the longest x1 31.2 us: local(): pl.pallas_call(lambda *refs: main_kernel(counts, *refs), out_shape=[pltpu...]
    unnamed x0 -> x8, local copies, waits for them, and re-layouts: none -> 3.09 us
where the time goes in v1:
time: 37.8 us; the launch traced here: 37.6 us
  Pallas kernels  33.9 us (90%)
  local copies, waits for them, and re-layouts  3.09 us (8%)
  between operations  0.65 us (2%)
    pallas_call x1, Pallas kernels, local(): pl.pallas_call(lambda *refs: main_kernel(counts, *refs), out_shape=[pltpu...  31.2 us
    unnamed x8, local copies, waits for them, and re-layouts  3.09 us
    pallas_call x1, Pallas kernels, local(): pl.pallas_call(drain_kernel, out_shape=[jax.ShapeDtypeStruct(s, F32) for...  2.71 us

profile of v1, /device:TPU:0, one launch (start us, length us, event | category | flops | bytes accessed | tf_op | source)
XLA Modules:
  0.0 37.6 jit_solution(761737002022693536)
XLA Ops:
  0.6 31.2 %main.1 = (f32[2,8,32,256]{3,2,1,0:T(8,128)S(1)}, f32[8,32,256]{2,1,0:T(8,128)S(1)}, f32[8,32,256]{2,1,0:T(8,128)S(1)}, f32[3,8,32,256]{3,2,1,0:T(8,128)S(1)}) custom-call(f32[3,8,32,256]{3,2,1,0:T(8,128)} %refs_0_.1, f32[8,32,256]{2,1,0:T(8,128)} %refs_1_.1, f32[3,8,32,256]{3,2,1,0:T(8,128)} %refs_2_.1, f32[8,32,256]{2,1,0:T(8,128)} %refs_3_.1, ...), custom_call_target="tpu_custom_call" | custom-call | tf_op jit(solution)/shard_map/main/pallas_call | solution.py:472
  31.8 0.0 copy-start
  31.8 0.9 %copy-done = f32[3,8,32,256]{3,2,1,0:T(8,128)} copy-done((f32[3,8,32,256]{3,2,1,0:T(8,128)}, f32[3,8,32,256]{3,2,1,0:T(8,128)S(1)}, u32[]{:S(2)}) %copy-start) | copy-done | bytes 786456
  32.7 0.0 copy-start.1
  32.7 0.8 %copy-done.1 = f32[2,8,32,256]{3,2,1,0:T(8,128)} copy-done((f32[2,8,32,256]{3,2,1,0:T(8,128)}, f32[2,8,32,256]{3,2,1,0:T(8,128)S(1)}, u32[]{:S(2)}) %copy-start.1) | copy-done | bytes 524312
  33.5 0.0 copy-start.2
  33.5 0.7 %copy-done.2 = f32[8,32,256]{2,1,0:T(8,128)} copy-done((f32[8,32,256]{2,1,0:T(8,128)}, f32[8,32,256]{2,1,0:T(8,128)S(1)}, u32[]{:S(2)}) %copy-start.2) | copy-done | bytes 262168
  34.2 0.0 copy-start.3
  34.2 0.7 %copy-done.3 = f32[8,32,256]{2,1,0:T(8,128)} copy-done((f32[8,32,256]{2,1,0:T(8,128)}, f32[8,32,256]{2,1,0:T(8,128)S(1)}, u32[]{:S(2)}) %copy-start.3) | copy-done | bytes 262168
  34.9 2.7 %drain.1 = (f32[2,8,32,256]{3,2,1,0:T(8,128)}, f32[8,32,256]{2,1,0:T(8,128)}, f32[8,32,256]{2,1,0:T(8,128)}, f32[3,8,32,256]{3,2,1,0:T(8,128)}) custom-call(f32[2,8,32,256]{3,2,1,0:T(8,128)} %copy-done.1, f32[8,32,256]{2,1,0:T(8,128)} %copy-done.2, f32[8,32,256]{2,1,0:T(8,128)} %copy-done.3, f32[3,8,32,256]{3,2,1,0:T(8,128)} %copy-done), custom_call_target="tpu_custom_call" | custom-call | tf_op jit(solution)/shard_map/drain/pallas_call | solution.py:496
Async XLA Ops:
  31.8 0.9 %copy-start = (f32[3,8,32,256]{3,2,1,0:T(8,128)}, f32[3,8,32,256]{3,2,1,0:T(8,128)S(1)}, u32[]{:S(2)}) copy-start(f32[3,8,32,256]{3,2,1,0:T(8,128)S(1)} %get-tuple-element.11.refs_3_) | copy-start | bytes 2359300
  32.7 0.8 %copy-start.1 = (f32[2,8,32,256]{3,2,1,0:T(8,128)}, f32[2,8,32,256]{3,2,1,0:T(8,128)S(1)}, u32[]{:S(2)}) copy-start(f32[2,8,32,256]{3,2,1,0:T(8,128)S(1)} %get-tuple-element.8.refs_0_) | copy-start | bytes 1572868
  33.5 0.7 %copy-start.2 = (f32[8,32,256]{2,1,0:T(8,128)}, f32[8,32,256]{2,1,0:T(8,128)S(1)}, u32[]{:S(2)}) copy-start(f32[8,32,256]{2,1,0:T(8,128)S(1)} %get-tuple-element.9.refs_1_) | copy-start | bytes 786436
  34.2 0.7 %copy-start.3 = (f32[8,32,256]{2,1,0:T(8,128)}, f32[8,32,256]{2,1,0:T(8,128)S(1)}, u32[]{:S(2)}) copy-start(f32[8,32,256]{2,1,0:T(8,128)S(1)} %get-tuple-element.10.refs_2_) | copy-start | bytes 786436

commit v2 on v1

--- a/solution.py
+++ b/solution.py
@@ -25,6 +25,10 @@
     return pltpu.roll(x, shift % n, axis) if shift % n else x
 
 
+def pick(x, index):
+    return jnp.take_along_axis(x, index, axis=1)
+
+
 def span(r, c):
     return (slice(r * SUB, (r + 1) * SUB), slice(c * LANE, (c + 1) * LANE))
 
@@ -40,7 +44,7 @@
         return self.memo[key]
 
 
-def chain(grid, v, h, t, g, dist, ew, kt, ct, swap=lambda i, f: f):
+def chain(grid, v, h, t, g, dist, ew, kt, ct, swap=lambda i, f: f, staged=False):
     sub, lane = iotas()
 
     def lift(fn, *fields):
@@ -72,8 +76,17 @@
         h1 = lift(mix, kt[3], kt[4], kt[5], hh, hc, hd)
         return (c0, c1), (h0, h1)
 
+    def now(*fs):
+        if staged:
+            for f in fs:
+                for r in range(grid[0]):
+                    for c in range(grid[1]):
+                        f(r, c)
+
+    now(*v, h, *t, g)
     cv, hv = parts(v, h)
     cw, hw = parts(t, g)
+    now(*cv, *hv, *cw, *hw)
 
     def potential(k):
         def make(r, c):
@@ -93,6 +106,7 @@
 
     p0, q0 = potential(0)
     p1, q1 = potential(1)
+    now(p0, q0, p1, q1)
     add = lambda a, b: a + b
     add3 = lambda a, b, c: a + b + c
 
@@ -106,12 +120,14 @@
     dd = cell(q0, q1)[0]
     cc, dd = swap(0, cc), swap(1, dd)
     p1_low = col_shift(p1_down, -1)
+    now(cc, dd, p1_low)
 
     def neighbours(f):
         fc = col_shift(f, 1)
         return row_shift(f, 1), fc, row_shift(fc, -1)
 
     cn, dn = neighbours(cc), neighbours(dd)
+    now(*cn, *dn)
     ends = [lift(add, p0, p1_low), pair, lift(add, p1, p0_up)]
     en = [
         lift(lambda w, a, b: w * (a * (a + b) + (1.0 / 3.0) * (b * b)), ew[k], v[k], t[k])
@@ -119,6 +135,7 @@
     ]
     e_up = row_shift(en[0], -1)
     e_low = col_shift(lift(add, en[1], row_shift(en[2], 1)), -1)
+    now(e_low)
 
     def outputs(scale):
         def edge(k):
@@ -274,23 +291,16 @@
         for c in range(nc):
             put_geo(geo, span(r, c), [f(*span(r, c)) for f in own_geo], b_area[span(r, c)])
 
-    def strip(fl, ft, l):
-        m = jnp.where(lane < 5, fl, roll(ft, 9, 1))
-        return roll(m, l * GROUP + 2, 1)
-
-    def spread(x):
-        for w in (GROUP, 2 * GROUP, 4 * GROUP):
-            x = jnp.where(lane < w, x, roll(x, w, 1))
-        return x
+    near_index = jnp.where(pos < 5, jnp.maximum(pos - 2, 0), jnp.minimum(pos + LANE - 11, LANE - 1))
+
+    def strip(f, rs):
+        return pick(jnp.where(lane < LANE // 2, f(rs, head), f(rs, tail)), near_index)
 
     def strip_levels(src, rs):
-        out = []
-        for k in range(8):
-            acc = jnp.zeros((SUB, LANE), F32)
-            for l in range(levels):
-                f = level_views(l, src)[k]
-                acc = jnp.where(group == l, strip(f(rs, head), f(rs, tail), l), acc)
-            out.append(acc)
+        got = [[strip(f, rs) for f in level_views(l, src)] for l in range(levels)]
+        out = got[0]
+        for l in range(1, levels):
+            out = [jnp.where(group == l, x, y) for x, y in zip(got[l], out)]
         return out
 
     for r in range(nr):
@@ -298,8 +308,8 @@
         for k, x in enumerate(strip_levels(bufs[:4], rs)):
             slev[k, rs] = x
         for k, f in enumerate(own_geo):
-            sgeo[k, rs] = strip(f(rs, head), f(rs, tail), 0)
-        sgeo[14, rs] = spread(strip(b_area[rs, head], b_area[rs, tail], 0))
+            sgeo[k, rs] = strip(f, rs)
+        sgeo[14, rs] = strip(view(b_area), rs)
 
     def fields(grid, views):
         return [Field(grid, lambda r, c, f=f: f(*span(r, c))) for f in views]
@@ -397,60 +407,61 @@
 
     low = slice(0, SUB)
     edge_rows = slice(rows, rows + SUB)
-    for k, x in enumerate(strip_levels(bands[:4], low)):
-        slev[k, edge_rows] = turn(x)
-    for k, f in enumerate(band_geo):
-        sgeo[k, edge_rows] = turn(strip(f(low, head), f(low, tail), 0))
-
-    def insert(x, k, rs, cs):
-        rt = roll(g_right[rs, cs], 11 - 2 * k, 1)
-        lt = roll(g_left[rs, cs], 2 - 2 * k, 1)
-        return jnp.where((pos == 11) | (pos == 12), rt, jnp.where(pos == 1, lt, x))
-
-    for r in range(nr + 1):
-        rs = slice(r * SUB, (r + 1) * SUB)
-        raw = [
-            spread(insert(sgeo[k, rs], k, rs, slice(LANE, 2 * LANE))) for k in range(14)
-        ]
-        for k in list(range(3)) + list(range(6, 12)):
-            sgeo[k, rs] = raw[k]
-        ws = [0.25 * raw[k] * raw[3 + k] for k in range(3)]
-        ts = [raw[12 + v] * (raw[6 + 3 * v] + raw[7 + 3 * v] + raw[8 + 3 * v]) for v in range(2)]
-        for k, x in zip((3, 4, 5, 12, 13), ws + ts):
-            sgeo[k, rs] = x
+    right_pos, left_pos = (pos == 11) | (pos == 12), pos == 1
+    tiles = [slice(r * SUB, (r + 1) * SUB) for r in range(nr + 1)]
+    band_levels = [turn(x) for x in strip_levels(bands[:4], low)]
+    band_near = [turn(strip(f, low)) for f in band_geo]
+    last = slice(LANE, 2 * LANE)
+
+    def insert_geo(k, r):
+        rt = pick(g_right[tiles[r], last], jnp.where(pos == 12, 2 * k + 1, 2 * k))
+        lt = pick(g_left[tiles[r], last], jnp.full((SUB, LANE), (2 * k - 1) % LANE, jnp.int32))
+        own_part = band_near[k] if r == nr else sgeo[k, tiles[r]]
+        return jnp.where(right_pos, rt, jnp.where(left_pos, lt, own_part))
+
+    def insert(k, r):
+        rt = roll(g_right[tiles[r], head], 11 - 2 * k, 1)
+        lt = roll(g_left[tiles[r], head], 2 - 2 * k, 1)
+        own_part = band_levels[k] if r == nr else slev[k, tiles[r]]
+        return jnp.where(right_pos, rt, jnp.where(left_pos, lt, own_part))
 
     grid = (nr + 1, 1)
-    one = lambda r: slice(r * SUB, (r + 1) * SUB)
-    sfield = lambda k: Field(grid, lambda r, c: sgeo[k, one(r)])
-    x = [
-        Field(grid, lambda r, c, k=k: insert(slev[k, one(r)], k, one(r), slice(0, LANE)))
-        for k in range(8)
-    ]
+    x = [Field(grid, lambda r, c, k=k: insert(k, r)) for k in range(8)]
+    raw = [Field(grid, lambda r, c, k=k: insert_geo(k, r)) for k in range(14)]
+    for f in x + raw:
+        for r in range(nr + 1):
+            f(r, 0)
+    ws = [Field(grid, lambda r, c, k=k: 0.25 * raw[k](r, c) * raw[3 + k](r, c)) for k in range(3)]
+
+    def weighed(v):
+        a = [raw[6 + 3 * v + k] for k in range(3)]
+        return Field(grid, lambda r, c: raw[12 + v](r, c) * (a[0](r, c) + a[1](r, c) + a[2](r, c)))
+
     outputs = chain(
-        grid, x[0:3], x[3], x[4:7], x[7],
-        [sfield(k) for k in range(3)],
-        [sfield(k) for k in (3, 4, 5)],
-        [sfield(k) for k in range(6, 12)],
-        [sfield(k) for k in (12, 13)],
+        grid, x[0:3], x[3], x[4:7], x[7], raw[0:3], ws, raw[6:12], [weighed(v) for v in range(2)],
+        staged=True,
     )[2]
-    scale = [Field(grid, lambda r, c, k=k: SLOPE / sgeo[k, one(r)]) for k in range(3)]
-    scale.append(Field(grid, lambda r, c: 1.0 / sgeo[14, one(r)]))
+    scale = [Field(grid, lambda r, c, k=k: SLOPE / raw[k](r, c)) for k in range(3)]
+    scale.append(Field(grid, lambda r, c: 1.0 / sgeo[14, tiles[r]]))
     outs = outputs(scale)
     refs_of = [(o_vert, (0,)), (o_vert, (1,)), (o_kin, ()), (o_cell, ())]
     refs_of += [(o_edge, (k,)) for k in range(3)]
     first, ends = lane == 0, lane >= LANE - 2
     end = lane == LANE - 1
     masks = [(None, end), (None, end), (first, None), (first, end), (first, ends), (first, ends), (first, ends)]
+    back = [
+        jnp.where(lane < LANE // 2, l * GROUP + 2, l * GROUP + 11 - LANE + lane) & (LANE - 1)
+        for l in range(levels)
+    ]
+    done = [[f(r, 0) for f in outs] for r in range(nr)]
     for r in range(nr):
-        for (ref, lead), f, (mf, me) in zip(refs_of, outs, masks):
-            y = f(r, 0)
-            y = jnp.where(pos == 2, y, roll(y, -9, 1))
-            for l in range(levels):
-                z = roll(y, -(l * GROUP + 2), 1)
+        moved = [[pick(y, back[l]) for l in range(levels)] for y in done[r]]
+        for (ref, lead), zs, (mf, me) in zip(refs_of, moved, masks):
+            for l, z in enumerate(zs):
                 if mf is not None:
-                    pltpu.store(ref.at[lead + (l, one(r), head)], z, mask=mf)
+                    pltpu.store(ref.at[lead + (l, tiles[r], head)], z, mask=mf)
                 if me is not None:
-                    pltpu.store(ref.at[lead + (l, one(r), tail)], z, mask=me)
+                    pltpu.store(ref.at[lead + (l, tiles[r], tail)], z, mask=me)
 
 
 def drain_kernel(*refs):
@@ -497,7 +508,7 @@
         drain_kernel,
         out_shape=[jax.ShapeDtypeStruct(s, F32) for s in outs],
         in_specs=[vmem] * len(outs),
-        out_specs=[hbm] * len(outs),
+        out_specs=[pl.BlockSpec(memory_space=pltpu.HBM)] * len(outs),
         scratch_shapes=[pltpu.SemaphoreType.DMA((len(outs),))],
         name="drain",
     )(*kept)

time: 37.8 us -> 20.8 us (0.55)
  Pallas kernels: 33.9 us -> 16.9 us
    pallas_call x1, Pallas kernels: 31.2 us -> 14.2 us  [local(): pl.pallas_call(lambda *refs: main_kernel(counts, *refs), out_shape=[pltpu...]
where the time goes in v2:
time: 20.8 us; the launch traced here: 20.7 us
  Pallas kernels  16.9 us (81%)
  local copies, waits for them, and re-layouts  3.09 us (15%)
  between operations  0.65 us (3%)
    pallas_call x1, Pallas kernels, local(): pl.pallas_call(lambda *refs: main_kernel(counts, *refs), out_shape=[pltpu...  14.2 us
    unnamed x8, local copies, waits for them, and re-layouts  3.09 us
    pallas_call x1, Pallas kernels, local(): pl.pallas_call(drain_kernel, out_shape=[jax.ShapeDtypeStruct(s, F32) for...  2.71 us

profile of v2, /device:TPU:0, one launch (start us, length us, event | category | flops | bytes accessed | tf_op | source)
XLA Modules:
  0.0 20.7 jit_solution(10084321670718347983)
XLA Ops:
  0.6 14.2 %main.1 = (f32[2,8,32,256]{3,2,1,0:T(8,128)S(1)}, f32[8,32,256]{2,1,0:T(8,128)S(1)}, f32[8,32,256]{2,1,0:T(8,128)S(1)}, f32[3,8,32,256]{3,2,1,0:T(8,128)S(1)}) custom-call(f32[3,8,32,256]{3,2,1,0:T(8,128)} %refs_0_.1, f32[8,32,256]{2,1,0:T(8,128)} %refs_1_.1, f32[3,8,32,256]{3,2,1,0:T(8,128)} %refs_2_.1, f32[8,32,256]{2,1,0:T(8,128)} %refs_3_.1, ...), custom_call_target="tpu_custom_call" | custom-call | tf_op jit(solution)/shard_map/main/pallas_call | solution.py:483
  14.8 0.0 copy-start
  14.9 0.9 %copy-done = f32[3,8,32,256]{3,2,1,0:T(8,128)} copy-done((f32[3,8,32,256]{3,2,1,0:T(8,128)}, f32[3,8,32,256]{3,2,1,0:T(8,128)S(1)}, u32[]{:S(2)}) %copy-start) | copy-done | bytes 786456
  15.7 0.0 copy-start.1
  15.7 0.8 %copy-done.1 = f32[2,8,32,256]{3,2,1,0:T(8,128)} copy-done((f32[2,8,32,256]{3,2,1,0:T(8,128)}, f32[2,8,32,256]{3,2,1,0:T(8,128)S(1)}, u32[]{:S(2)}) %copy-start.1) | copy-done | bytes 524312
  16.5 0.0 copy-start.2
  16.5 0.7 %copy-done.2 = f32[8,32,256]{2,1,0:T(8,128)} copy-done((f32[8,32,256]{2,1,0:T(8,128)}, f32[8,32,256]{2,1,0:T(8,128)S(1)}, u32[]{:S(2)}) %copy-start.2) | copy-done | bytes 262168
  17.2 0.0 copy-start.3
  17.2 0.7 %copy-done.3 = f32[8,32,256]{2,1,0:T(8,128)} copy-done((f32[8,32,256]{2,1,0:T(8,128)}, f32[8,32,256]{2,1,0:T(8,128)S(1)}, u32[]{:S(2)}) %copy-start.3) | copy-done | bytes 262168
  17.9 2.7 %drain.1 = (f32[2,8,32,256]{3,2,1,0:T(8,128)}, f32[8,32,256]{2,1,0:T(8,128)}, f32[8,32,256]{2,1,0:T(8,128)}, f32[3,8,32,256]{3,2,1,0:T(8,128)}) custom-call(f32[2,8,32,256]{3,2,1,0:T(8,128)} %copy-done.1, f32[8,32,256]{2,1,0:T(8,128)} %copy-done.2, f32[8,32,256]{2,1,0:T(8,128)} %copy-done.3, f32[3,8,32,256]{3,2,1,0:T(8,128)} %copy-done), custom_call_target="tpu_custom_call" | custom-call | tf_op jit(solution)/shard_map/drain/pallas_call | solution.py:507
Async XLA Ops:
  14.8 0.9 %copy-start = (f32[3,8,32,256]{3,2,1,0:T(8,128)}, f32[3,8,32,256]{3,2,1,0:T(8,128)S(1)}, u32[]{:S(2)}) copy-start(f32[3,8,32,256]{3,2,1,0:T(8,128)S(1)} %get-tuple-element.11.refs_3_) | copy-start | bytes 2359300
  15.7 0.8 %copy-start.1 = (f32[2,8,32,256]{3,2,1,0:T(8,128)}, f32[2,8,32,256]{3,2,1,0:T(8,128)S(1)}, u32[]{:S(2)}) copy-start(f32[2,8,32,256]{3,2,1,0:T(8,128)S(1)} %get-tuple-element.8.refs_0_) | copy-start | bytes 1572868
  16.5 0.7 %copy-start.2 = (f32[8,32,256]{2,1,0:T(8,128)}, f32[8,32,256]{2,1,0:T(8,128)S(1)}, u32[]{:S(2)}) copy-start(f32[8,32,256]{2,1,0:T(8,128)S(1)} %get-tuple-element.9.refs_1_) | copy-start | bytes 786436
  17.2 0.7 %copy-start.3 = (f32[8,32,256]{2,1,0:T(8,128)}, f32[8,32,256]{2,1,0:T(8,128)S(1)}, u32[]{:S(2)}) copy-start(f32[8,32,256]{2,1,0:T(8,128)S(1)} %get-tuple-element.10.refs_2_) | copy-start | bytes 786436

commit v3 on v2

--- a/solution.py
+++ b/solution.py
@@ -9,6 +9,7 @@
 LANE = 128
 GROUP = 16
 PAIR = 2
+BATCH = 8
 MESH = pl.DeviceIdType.MESH
 F32 = jnp.float32
 SLOPE = -0.5 / 36.0
@@ -44,7 +45,7 @@
         return self.memo[key]
 
 
-def chain(grid, v, h, t, g, dist, ew, kt, ct, swap=lambda i, f: f, staged=False):
+def chain(grid, v, h, t, g, dist, ew, kt, ct, swap=lambda i, f: f):
     sub, lane = iotas()
 
     def lift(fn, *fields):
@@ -76,17 +77,8 @@
         h1 = lift(mix, kt[3], kt[4], kt[5], hh, hc, hd)
         return (c0, c1), (h0, h1)
 
-    def now(*fs):
-        if staged:
-            for f in fs:
-                for r in range(grid[0]):
-                    for c in range(grid[1]):
-                        f(r, c)
-
-    now(*v, h, *t, g)
     cv, hv = parts(v, h)
     cw, hw = parts(t, g)
-    now(*cv, *hv, *cw, *hw)
 
     def potential(k):
         def make(r, c):
@@ -106,7 +98,6 @@
 
     p0, q0 = potential(0)
     p1, q1 = potential(1)
-    now(p0, q0, p1, q1)
     add = lambda a, b: a + b
     add3 = lambda a, b, c: a + b + c
 
@@ -120,14 +111,12 @@
     dd = cell(q0, q1)[0]
     cc, dd = swap(0, cc), swap(1, dd)
     p1_low = col_shift(p1_down, -1)
-    now(cc, dd, p1_low)
 
     def neighbours(f):
         fc = col_shift(f, 1)
         return row_shift(f, 1), fc, row_shift(fc, -1)
 
     cn, dn = neighbours(cc), neighbours(dd)
-    now(*cn, *dn)
     ends = [lift(add, p0, p1_low), pair, lift(add, p1, p0_up)]
     en = [
         lift(lambda w, a, b: w * (a * (a + b) + (1.0 / 3.0) * (b * b)), ew[k], v[k], t[k])
@@ -135,7 +124,6 @@
     ]
     e_up = row_shift(en[0], -1)
     e_low = col_shift(lift(add, en[1], row_shift(en[2], 1)), -1)
-    now(e_low)
 
     def outputs(scale):
         def edge(k):
@@ -156,7 +144,8 @@
             lift(lambda a: a * (1.0 / 36.0), cc),
         ] + [edge(k) for k in range(3)]
 
-    return cc, dd, outputs
+    stages = [[*cv, *hv, *cw, *hw, e_low], [p0, q0, p1, q1], [cc, dd, p1_low], [*cn, *dn]]
+    return cc, dd, outputs, stages
 
 
 def main_kernel(counts, *refs):
@@ -187,12 +176,9 @@
     pos, group = lane & (GROUP - 1), lane >> 4
     head, tail = slice(0, LANE), slice(cols - LANE, cols)
 
-    loads = [pltpu.make_async_copy(a, b, in_sem.at[i]) for i, (a, b) in enumerate(zip(hbm, bufs))]
-    for i in (4, 5, 6, 7, 0, 1, 2, 3, 8):
-        loads[i].start()
-
-    def part(ref, a, b):
-        return ref.at[(slice(None),) * (len(ref.shape) - 2) + (slice(a, b), slice(None))]
+    def part(ref, a, b, *lead):
+        rest = (slice(None),) * (len(ref.shape) - 2 - len(lead))
+        return ref.at[lead + rest + (slice(a, b), slice(None))]
 
     own = []
     for i, (a, b) in enumerate(zip(hbm, bands)):
@@ -200,6 +186,9 @@
         own.append(pltpu.make_async_copy(part(a, 0, 2), part(b, 6, 8), own_sem.at[2 * i + 1]))
     for copy in own:
         copy.start()
+    loads = [pltpu.make_async_copy(a, b, in_sem.at[i]) for i, (a, b) in enumerate(zip(hbm, bufs))]
+    for i in (4, 5, 6, 7, 0, 1, 2, 3, 8):
+        loads[i].start()
 
     def remote(src, dst, sems, i, y, x):
         return pltpu.make_async_remote_copy(
@@ -211,11 +200,25 @@
             device_id_type=MESH,
         )
 
+    vel, th, vt, tt, cd, el, kite, cor = bands[:8]
+    to_up = [
+        (2, vel, slice(1, 3)), (1, vel, 0), (2, th), (2, vt, slice(1, 3)), (1, vt, 0), (2, tt),
+        (2, cd, slice(1, 3)), (1, cd, 0), (1, el, 2), (2, kite, 1), (1, kite, 0), (2, cor, 1), (1, cor, 0),
+    ]
+    to_down = [
+        (2, vel, slice(0, 2)), (1, vel, 2), (2, th), (2, vt, slice(0, 2)), (1, vt, 2), (2, tt),
+        (2, cd, slice(0, 2)), (1, cd, 2), (1, el, 0), (2, kite, 0), (1, kite, 1), (2, cor, 0), (1, cor, 1),
+    ]
+    sems = (send_row, recv_row)
     row_copies = []
-    for i, (a, b) in enumerate(zip(hbm[:8], bands)):
-        sems = (send_row, recv_row)
-        row_copies.append(remote(part(a, 0, 2), part(b, 2, 4), sems, 2 * i, up, px))
-        row_copies.append(remote(part(a, rows - 2, rows), part(b, 4, 6), sems, 2 * i + 1, down, px))
+    for i, (n, b, *lead) in enumerate(to_up):
+        lead = tuple(lead)
+        row_copies.append(remote(part(b, 6, 6 + n, *lead), part(b, 2, 2 + n, *lead), sems, i, up, px))
+    for i, (n, b, *lead) in enumerate(to_down):
+        lead, i = tuple(lead), i + len(to_up)
+        row_copies.append(remote(part(b, 2 - n, 2, *lead), part(b, 6 - n, 6, *lead), sems, i, down, px))
+    for copy in own:
+        copy.wait()
     pl.semaphore_wait(barrier, len(near))
     for copy in row_copies:
         copy.start()
@@ -317,14 +320,14 @@
     def run(grid, x, kites, dist, derived, swap=lambda i, f: f):
         f = fields(grid, derived)
         d = fields(grid, dist)
-        cc, dd, outputs = chain(
+        cc, dd, outputs, stages = chain(
             grid, x[0:3], x[3], x[4:7], x[7], d, f[0:3], fields(grid, kites), f[3:5], swap
         )
-        return cc, dd, outputs(f[5:9])
+        return cc, dd, outputs(f[5:9]), stages
 
     def block(l):
         grid = (nr, nc)
-        cc, dd, outs = run(
+        cc, dd, outs, _ = run(
             grid,
             fields(grid, level_views(l, bufs[:4])),
             own_geo[6:12],
@@ -356,18 +359,9 @@
 
     lax.fori_loop(0, levels // PAIR, inner, 0)
 
-    for copy in own:
-        copy.wait()
-    for copy in row_copies + col_copies:
-        copy.wait()
-
     band_geo = geo_views(bands[4:8])
-    for c in range(nc):
-        at = span(0, c)
-        put_geo(kgeo, at, [f(*at) for f in band_geo], bands[8][at])
-
     merge = (sub == 0) | (sub == SUB - 1)
-    for l in range(levels):
+    def border_rows(l):
         grid = (1, nc)
 
         def swap(i, f, l=l):
@@ -375,14 +369,14 @@
                 grid, lambda r, c: jnp.where(merge, saved[i, l, :, span(0, c)[1]], f(r, c))
             )
 
-        outs = run(
+        outs, stages = run(
             grid,
             fields(grid, level_views(l, bands[:4])),
             band_geo[6:12],
             band_geo[0:3],
             [view(kgeo, k) for k in range(9)],
             swap,
-        )[2]
+        )[2:]
         dst = [(o_vert, (0, l)), (o_vert, (1, l)), (o_kin, (l,)), (o_cell, (l,))]
         dst += [(o_edge, (k, l)) for k in range(3)]
         both = ((rows - 1, 1, 1), (0, 6, 1))
@@ -395,12 +389,16 @@
             both,
             ((rows - 1, 1, 1), (0, 6, 2)),
         ]
-        for c in range(nc):
-            cs = span(0, c)[1]
-            for (ref, lead), f, ranges in zip(dst, outs, which):
-                x = f(0, c)
-                for to, src, n in ranges:
-                    ref[lead + (slice(to, to + n), cs)] = x[src : src + n]
+
+        def put():
+            for c in range(nc):
+                cs = span(0, c)[1]
+                for (ref, lead), f, ranges in zip(dst, outs, which):
+                    x = f(0, c)
+                    for to, src, n in ranges:
+                        ref[lead + (slice(to, to + n), cs)] = x[src : src + n]
+
+        return stages, put
 
     def turn(x):
         return jnp.where(sub < 4, roll(x, -2, 0), roll(x, 2, 0))
@@ -409,41 +407,72 @@
     edge_rows = slice(rows, rows + SUB)
     right_pos, left_pos = (pos == 11) | (pos == 12), pos == 1
     tiles = [slice(r * SUB, (r + 1) * SUB) for r in range(nr + 1)]
-    band_levels = [turn(x) for x in strip_levels(bands[:4], low)]
-    band_near = [turn(strip(f, low)) for f in band_geo]
     last = slice(LANE, 2 * LANE)
 
     def insert_geo(k, r):
         rt = pick(g_right[tiles[r], last], jnp.where(pos == 12, 2 * k + 1, 2 * k))
         lt = pick(g_left[tiles[r], last], jnp.full((SUB, LANE), (2 * k - 1) % LANE, jnp.int32))
-        own_part = band_near[k] if r == nr else sgeo[k, tiles[r]]
+        own_part = edge_geo[k] if r == nr else sgeo[k, tiles[r]]
         return jnp.where(right_pos, rt, jnp.where(left_pos, lt, own_part))
 
     def insert(k, r):
         rt = roll(g_right[tiles[r], head], 11 - 2 * k, 1)
         lt = roll(g_left[tiles[r], head], 2 - 2 * k, 1)
-        own_part = band_levels[k] if r == nr else slev[k, tiles[r]]
+        own_part = edge_levels[k] if r == nr else slev[k, tiles[r]]
         return jnp.where(right_pos, rt, jnp.where(left_pos, lt, own_part))
 
     grid = (nr + 1, 1)
     x = [Field(grid, lambda r, c, k=k: insert(k, r)) for k in range(8)]
     raw = [Field(grid, lambda r, c, k=k: insert_geo(k, r)) for k in range(14)]
-    for f in x + raw:
-        for r in range(nr + 1):
-            f(r, 0)
     ws = [Field(grid, lambda r, c, k=k: 0.25 * raw[k](r, c) * raw[3 + k](r, c)) for k in range(3)]
 
     def weighed(v):
         a = [raw[6 + 3 * v + k] for k in range(3)]
         return Field(grid, lambda r, c: raw[12 + v](r, c) * (a[0](r, c) + a[1](r, c) + a[2](r, c)))
 
-    outputs = chain(
+    _, _, outputs, stages = chain(
         grid, x[0:3], x[3], x[4:7], x[7], raw[0:3], ws, raw[6:12], [weighed(v) for v in range(2)],
-        staged=True,
-    )[2]
+    )
     scale = [Field(grid, lambda r, c, k=k: SLOPE / raw[k](r, c)) for k in range(3)]
     scale.append(Field(grid, lambda r, c: 1.0 / sgeo[14, tiles[r]]))
     outs = outputs(scale)
+    own_tiles = range(nr)
+
+    def build(fields_of, at, across=(0,)):
+        for f in fields_of:
+            for r in at:
+                for c in across:
+                    f(r, c)
+
+    edge_levels, edge_geo = [], []
+    for copy in col_copies[:2]:
+        copy.wait()
+    build(x + raw, own_tiles)
+    cv, hv, cw, hw = (stages[0][2 * i : 2 * i + 2] for i in range(4))
+    build([cv[0], hv[0], cw[0], hw[0]], range(nr - 1))
+    build([cv[1], hv[1], cw[1], hw[1]], range(1, nr))
+    build(stages[1][:2], range(nr - 1))
+    build(stages[1][2:], range(1, nr))
+    build(stages[2][:2], range(1, nr - 1))
+
+    for copy in row_copies + col_copies[2:]:
+        copy.wait()
+    edge_levels += [turn(f) for f in strip_levels(bands[:4], low)]
+    edge_geo += [turn(strip(f, low)) for f in band_geo]
+    for c in range(nc):
+        at = span(0, c)
+        put_geo(kgeo, at, [f(*at) for f in band_geo], bands[8][at])
+    build(x + raw, (nr,))
+    for start in range(0, levels, BATCH):
+        jobs = [border_rows(l) for l in range(start, start + BATCH)]
+        for i in range(len(stages)):
+            for kstages, _ in jobs:
+                build(kstages[i], (0,), range(nc))
+            if start + BATCH == levels:
+                build(stages[i], range(nr + 1))
+        for _, put in jobs:
+            put()
+    build(outs, own_tiles)
     refs_of = [(o_vert, (0,)), (o_vert, (1,)), (o_kin, ()), (o_cell, ())]
     refs_of += [(o_edge, (k,)) for k in range(3)]
     first, ends = lane == 0, lane >= LANE - 2
@@ -454,10 +483,10 @@
         for l in range(levels)
     ]
     done = [[f(r, 0) for f in outs] for r in range(nr)]
-    for r in range(nr):
-        moved = [[pick(y, back[l]) for l in range(levels)] for y in done[r]]
-        for (ref, lead), zs, (mf, me) in zip(refs_of, moved, masks):
-            for l, z in enumerate(zs):
+    for l in range(levels):
+        for r in range(nr):
+            moved = [pick(y, back[l]) for y in done[r]]
+            for (ref, lead), z, (mf, me) in zip(refs_of, moved, masks):
                 if mf is not None:
                     pltpu.store(ref.at[lead + (l, tiles[r], head)], z, mask=mf)
                 if me is not None:
@@ -496,8 +525,8 @@
             pltpu.VMEM((2, levels, SUB, cols), F32),
             pltpu.SemaphoreType.DMA((9,)),
             pltpu.SemaphoreType.DMA((18,)),
-            pltpu.SemaphoreType.DMA((16,)),
-            pltpu.SemaphoreType.DMA((16,)),
+            pltpu.SemaphoreType.DMA((26,)),
+            pltpu.SemaphoreType.DMA((26,)),
             pltpu.SemaphoreType.DMA((5,)),
             pltpu.SemaphoreType.DMA((5,)),
         ],
@@ -511,7 +540,7 @@
         out_specs=[pl.BlockSpec(memory_space=pltpu.HBM)] * len(outs),
         scratch_shapes=[pltpu.SemaphoreType.DMA((len(outs),))],
         name="drain",
-    )(*kept)
+    )(*[pltpu.with_memory_space_constraint(x, pltpu.VMEM) for x in kept])
 
 
 def solution(mesh):

time: 20.8 us -> 14.7 us (0.71)
  local copies, waits for them, and re-layouts: 3.09 us -> 0 us
  Pallas kernels: 16.9 us -> 13.9 us
    unnamed x8 -> x0, local copies, waits for them, and re-layouts: 3.09 us -> none
    pallas_call x1, Pallas kernels: 14.2 us -> 12.7 us  [local(): pl.pallas_call(lambda *refs: main_kernel(counts, *refs), out_shape=[pltpu...]
    pallas_call x1, Pallas kernels: 2.71 us -> 1.26 us  [local(): pl.pallas_call(drain_kernel, out_shape=[jax.ShapeDtypeStruct(s, F32) for...]
where the time goes in v3:
time: 14.7 us; the launch traced here: 14.6 us
  Pallas kernels  13.9 us (95%)
  between operations  0.64 us (4%)
    pallas_call x1, Pallas kernels, local(): pl.pallas_call(lambda *refs: main_kernel(counts, *refs), out_shape=[pltpu...  12.7 us
    pallas_call x1, Pallas kernels, local(): pl.pallas_call(drain_kernel, out_shape=[jax.ShapeDtypeStruct(s, F32) for...  1.26 us

profile of v3, /device:TPU:0, one launch (start us, length us, event | category | flops | bytes accessed | tf_op | source)
XLA Modules:
  0.0 14.6 jit_solution(350717489030121055)
XLA Ops:
  0.6 12.7 %main.1 = (f32[2,8,32,256]{3,2,1,0:T(8,128)S(1)}, f32[8,32,256]{2,1,0:T(8,128)S(1)}, f32[8,32,256]{2,1,0:T(8,128)S(1)}, f32[3,8,32,256]{3,2,1,0:T(8,128)S(1)}) custom-call(f32[3,8,32,256]{3,2,1,0:T(8,128)} %refs_0_.1, f32[8,32,256]{2,1,0:T(8,128)} %refs_1_.1, f32[3,8,32,256]{3,2,1,0:T(8,128)} %refs_2_.1, f32[8,32,256]{2,1,0:T(8,128)} %refs_3_.1, ...), custom_call_target="tpu_custom_call" | custom-call | tf_op jit(solution)/shard_map/main/pallas_call | solution.py:512
  13.3 1.3 %drain.1 = (f32[2,8,32,256]{3,2,1,0:T(8,128)}, f32[8,32,256]{2,1,0:T(8,128)}, f32[8,32,256]{2,1,0:T(8,128)}, f32[3,8,32,256]{3,2,1,0:T(8,128)}) custom-call(f32[2,8,32,256]{3,2,1,0:T(8,128)S(1)} %get-tuple-element.8.refs_0_, f32[8,32,256]{2,1,0:T(8,128)S(1)} %get-tuple-element.9.refs_1_, f32[8,32,256]{2,1,0:T(8,128)S(1)} %get-tuple-element.10.refs_2_, ...), custom_call_target="tpu_custom_call" | custom-call | tf_op jit(solution)/shard_map/drain/pallas_call | solution.py:536

commit v4 on v3

v4 whole, which is shorter than its diff:
```python
import jax
import jax.numpy as jnp
from jax import lax
from jax.experimental import pallas as pl
from jax.experimental.pallas import tpu as pltpu
from jax.sharding import PartitionSpec as P

SUB = 8
LANE = 128
GROUP = 16
PAIR = 2
MESH = pl.DeviceIdType.MESH
F32 = jnp.float32
SLOPE = -0.5 / 36.0


def iotas():
    sub = lax.broadcasted_iota(jnp.int32, (SUB, LANE), 0)
    lane = lax.broadcasted_iota(jnp.int32, (SUB, LANE), 1)
    return sub, lane


def roll(x, shift, axis):
    n = (SUB, LANE)[axis]
    return pltpu.roll(x, shift % n, axis) if shift % n else x


def pick(x, index):
    return jnp.take_along_axis(x, index, axis=1)


def span(r, c):
    return (slice(r * SUB, (r + 1) * SUB), slice(c * LANE, (c + 1) * LANE))


class Field:
    def __init__(self, grid, make):
        self.grid, self.make, self.memo = grid, make, {}

    def __call__(self, r, c):
        key = (r % self.grid[0], c % self.grid[1])
        if key not in self.memo:
            self.memo[key] = self.make(*key)
        return self.memo[key]


def chain(grid, v, h, t, g, dist, ew, kt, ct, swap=lambda i, f: f):
    sub, lane = iotas()

    def lift(fn, *fields):
        return Field(grid, lambda r, c: fn(*[f(r, c) for f in fields]))

    def row_shift(f, a):
        rolled = Field(grid, lambda r, c: roll(f(r, c), -a, 0))
        if grid[0] == 1:
            return rolled
        keep = sub < SUB - 1 if a == 1 else sub > 0
        return Field(grid, lambda r, c: jnp.where(keep, rolled(r, c), rolled(r + a, c)))

    def col_shift(f, b):
        rolled = Field(grid, lambda r, c: roll(f(r, c), -b, 1))
        if grid[1] == 1:
            return rolled
        keep = lane < LANE - 1 if b == 1 else lane > 0
        return Field(grid, lambda r, c: jnp.where(keep, rolled(r, c), rolled(r, c + b)))

    def parts(vv, hh):
        flux = [lift(lambda a, b: a * b, vv[k], dist[k]) for k in range(3)]
        c0 = lift(lambda a, b, c: a + b - c, flux[0], row_shift(flux[2], 1), flux[1])
        c1 = lift(lambda a, b, c: a - b - c, flux[1], flux[2], col_shift(row_shift(flux[0], -1), 1))
        hc = col_shift(hh, 1)
        hr = row_shift(hh, 1)
        hd = row_shift(hc, -1)
        mix = lambda a, b, c, p, q, s: a * p + b * q + c * s
        h0 = lift(mix, kt[0], kt[1], kt[2], hh, hr, hc)
        h1 = lift(mix, kt[3], kt[4], kt[5], hh, hc, hd)
        return (c0, c1), (h0, h1)

    cv, hv = parts(v, h)
    cw, hw = parts(t, g)

    def potential(k):
        def make(r, c):
            a0 = ct[k](r, c) + cv[k](r, c)
            a1 = cw[k](r, c)
            b0 = hv[k](r, c)
            b1 = hw[k](r, c)
            bm, be = b0 + 0.5 * b1, b0 + b1
            m = bm * be
            scale_all = 1.0 / (b0 * m)
            mid = (a0 + a0 + a1) * (b0 * be)
            late = mid + (a0 + a1) * (b0 * bm)
            return (a0 * m + mid + late) * scale_all, late * scale_all

        both = Field(grid, make)
        return Field(grid, lambda r, c: both(r, c)[0]), Field(grid, lambda r, c: both(r, c)[1])

    p0, q0 = potential(0)
    p1, q1 = potential(1)
    add = lambda a, b: a + b
    add3 = lambda a, b, c: a + b + c

    def cell(f0, f1):
        f0_up = row_shift(f0, -1)
        f1_down = row_shift(f1, 1)
        pair = lift(add, f0, f1)
        return lift(add3, pair, f0_up, col_shift(lift(add, pair, f1_down), -1)), f0_up, f1_down, pair

    cc, p0_up, p1_down, pair = cell(p0, p1)
    dd = cell(q0, q1)[0]
    cc, dd = swap(0, cc), swap(1, dd)
    p1_low = col_shift(p1_down, -1)

    def neighbours(f):
        fc = col_shift(f, 1)
        return row_shift(f, 1), fc, row_shift(fc, -1)

    cn, dn = neighbours(cc), neighbours(dd)
    ends = [lift(add, p0, p1_low), pair, lift(add, p1, p0_up)]
    en = [
        lift(lambda w, a, b: w * (a * (a + b) + (1.0 / 3.0) * (b * b)), ew[k], v[k], t[k])
        for k in range(3)
    ]
    e_up = row_shift(en[0], -1)
    e_low = col_shift(lift(add, en[1], row_shift(en[2], 1)), -1)

    def outputs(scale):
        def edge(k):
            def make(r, c):
                slope = v[k](r, c) * (cn[k](r, c) - cc(r, c)) + t[k](r, c) * (dn[k](r, c) - dd(r, c))
                return ends[k](r, c) * (1.0 / 12.0) + scale[k](r, c) * slope

            return Field(grid, make)

        kin = Field(
            grid,
            lambda r, c: (en[0](r, c) + en[1](r, c) + en[2](r, c) + e_up(r, c) + e_low(r, c)) * scale[3](r, c),
        )
        return [
            lift(lambda a: a * (1.0 / 6.0), p0),
            lift(lambda a: a * (1.0 / 6.0), p1),
            kin,
            lift(lambda a: a * (1.0 / 36.0), cc),
        ] + [edge(k) for k in range(3)]

    stages = [[*cv, *hv, *cw, *hw, e_low], [p0, q0, p1, q1], [cc, dd, p1_low], [*cn, *dn]]
    return cc, dd, outputs, stages


def view(ref, *lead):
    return lambda r, c: ref[lead + (r, c)]


def level_views(l, src):
    vel, th, vt, tt = src
    return (
        [view(vel, k, l) for k in range(3)]
        + [view(th, l)]
        + [view(vt, k, l) for k in range(3)]
        + [view(tt, l)]
    )


def geo_views(src):
    cd, el, kite, cor = src
    return (
        [view(cd, k) for k in range(3)]
        + [view(el, k) for k in range(3)]
        + [view(kite, v, k) for v in range(2) for k in range(3)]
        + [view(cor, v) for v in range(2)]
    )


def put_geo(dst, at, f, area):
    for k in range(3):
        dst[(k,) + at] = 0.25 * f[k] * f[3 + k]
        dst[(5 + k,) + at] = SLOPE / f[k]
    for v in range(2):
        dst[(3 + v,) + at] = f[12 + v] * (f[6 + 3 * v] + f[7 + 3 * v] + f[8 + 3 * v])
    dst[(8,) + at] = 1.0 / area


def fields(grid, views):
    return [Field(grid, lambda r, c, f=f: f(*span(r, c))) for f in views]


def run(grid, x, kites, dist, derived, swap=lambda i, f: f):
    f = fields(grid, derived)
    d = fields(grid, dist)
    cc, dd, outputs, stages = chain(
        grid, x[0:3], x[3], x[4:7], x[7], d, f[0:3], fields(grid, kites), f[3:5], swap
    )
    return cc, dd, outputs(f[5:9]), stages


def build(fields_of):
    for f in fields_of:
        for r in range(f.grid[0]):
            for c in range(f.grid[1]):
                f(r, c)


class Strips:
    def __init__(self, levels, cols):
        _, lane = iotas()
        self.levels, self.lane = levels, lane
        self.head, self.tail = slice(0, LANE), slice(cols - LANE, cols)
        pos = lane & (GROUP - 1)
        self.pos, self.group = pos, lane >> 4
        self.index = jnp.where(pos < 5, jnp.maximum(pos - 2, 0), jnp.minimum(pos + LANE - 11, LANE - 1))
        self.back = [
            jnp.where(lane < LANE // 2, l * GROUP + 2, l * GROUP + 11 - LANE + lane) & (LANE - 1)
            for l in range(levels)
        ]

    def own(self, f, rs):
        return pick(jnp.where(self.lane < LANE // 2, f(rs, self.head), f(rs, self.tail)), self.index)

    def own_levels(self, src, rs):
        got = [[self.own(f, rs) for f in level_views(l, src)] for l in range(self.levels)]
        out = got[0]
        for l in range(1, self.levels):
            out = [jnp.where(self.group == l, x, y) for x, y in zip(got[l], out)]
        return out

    def insert(self, x, right, left):
        pos = self.pos
        return jnp.where((pos == 11) | (pos == 12), right, jnp.where(pos == 1, left, x))

    def with_level(self, k, x, right, left):
        return self.insert(x, roll(right, 11 - 2 * k, 1), roll(left, 2 - 2 * k, 1))

    def with_geo(self, k, x, right, left):
        rt = pick(right, jnp.where(self.pos == 12, 2 * k + 1, 2 * k))
        lt = pick(left, jnp.full((SUB, LANE), (2 * k - 1) % LANE, jnp.int32))
        return self.insert(x, rt, lt)

    def masks(self):
        lane = self.lane
        first, end, ends = lane == 0, lane == LANE - 1, lane >= LANE - 2
        return [(None, end), (None, end), (first, None), (first, end)] + [(first, ends)] * 3


def strip_chain(grid, x, raw, area, swap=lambda i, f: f):
    ws = [Field(grid, lambda r, c, k=k: 0.25 * raw[k](r, c) * raw[3 + k](r, c)) for k in range(3)]

    def weighed(v):
        a = [raw[6 + 3 * v + k] for k in range(3)]
        return Field(grid, lambda r, c: raw[12 + v](r, c) * (a[0](r, c) + a[1](r, c) + a[2](r, c)))

    cc, dd, outputs, stages = chain(
        grid, x[0:3], x[3], x[4:7], x[7], raw[0:3], ws, raw[6:12], [weighed(v) for v in range(2)], swap
    )
    scale = [Field(grid, lambda r, c, k=k: SLOPE / raw[k](r, c)) for k in range(3)]
    scale.append(Field(grid, lambda r, c: 1.0 / area(r, c)))
    return cc, dd, outputs(scale), stages


def planes(vert, kin, cell, edge):
    return [(vert, (0,)), (vert, (1,)), (kin, ()), (cell, ())] + [(edge, (k,)) for k in range(3)]


def main_kernel(counts, *refs):
    hbm = refs[:9]
    o_vert, o_kin, o_cell, o_edge = refs[9:13]
    bands = refs[13:22]
    g_right, g_left, saved, ssaved = refs[22:26]
    bufs = refs[26:35]
    p_right, p_left, geo, slev, sgeo, tally = refs[35:41]
    in_sem, own_sem, send_row, recv_row, send_col, recv_col = refs[41:47]
    ny, nx = counts
    py, px = lax.axis_index("py"), lax.axis_index("px")
    down, up = lax.rem(py + 1, ny), lax.rem(py + ny - 1, ny)
    right, left = lax.rem(px + 1, nx), lax.rem(px + nx - 1, nx)

    barrier = pltpu.get_barrier_semaphore()
    near = [
        (up, px), (down, px), (py, left), (py, right),
        (up, left), (up, right), (down, left), (down, right),
    ]
    for y, x in near:
        pl.semaphore_signal(barrier, inc=1, device_id={"py": y, "px": x}, device_id_type=MESH)

    b_area = bufs[8]
    levels, rows, cols = bufs[1].shape
    nr, nc = rows // SUB, cols // LANE
    sub, lane = iotas()

    def await_rows(sem, n):
        pltpu.make_async_copy(tally.at[0:n], tally.at[0:n], sem).wait()

    def part(ref, a, b, *lead):
        rest = (slice(None),) * (len(ref.shape) - 2 - len(lead))
        return ref.at[lead + rest + (slice(a, b), slice(None))]

    def count(ref):
        n = 1
        for d in ref.shape[:-1]:
            n *= d
        return n

    own = []
    for a, b in zip(hbm, bands):
        own.append(pltpu.make_async_copy(part(a, rows - 2, rows), part(b, 0, 2), own_sem.at[0]))
        own.append(pltpu.make_async_copy(part(a, 0, 2), part(b, 6, 8), own_sem.at[0]))
    for copy in own:
        copy.start()
    own_rows = sum(4 * count(b) // SUB for b in bands)
    late = (4, 5, 6, 7, 8, 0, 1, 2, 3)
    for i in late:
        pltpu.make_async_copy(hbm[i], bufs[i], in_sem.at[0 if i >= 4 else 1]).start()

    def remote(src, dst, send, recv, y, x):
        return pltpu.make_async_remote_copy(
            src_ref=src,
            dst_ref=dst,
            send_sem=send,
            recv_sem=recv,
            device_id={"py": y, "px": x},
            device_id_type=MESH,
        )

    vel, th, vt, tt, cd, el, kite, cor = bands[:8]
    to_up = [
        (2, vel, slice(1, 3)), (1, vel, 0), (2, th), (2, vt, slice(1, 3)), (1, vt, 0), (2, tt),
        (2, cd, slice(1, 3)), (1, cd, 0), (1, el, 2), (2, kite, 1), (1, kite, 0), (2, cor, 1), (1, cor, 0),
    ]
    to_down = [
        (2, vel, slice(0, 2)), (1, vel, 2), (2, th), (2, vt, slice(0, 2)), (1, vt, 2), (2, tt),
        (2, cd, slice(0, 2)), (1, cd, 2), (1, el, 0), (2, kite, 0), (1, kite, 1), (2, cor, 0), (1, cor, 1),
    ]
    sems = (send_row.at[0], recv_row.at[0])
    row_copies, sent = [], 0
    for n, b, *lead in to_up:
        src = part(b, 6, 6 + n, *lead)
        row_copies.append(remote(src, part(b, 2, 2 + n, *lead), *sems, up, px))
        sent += count(src)
    for n, b, *lead in to_down:
        src = part(b, 2 - n, 2, *lead)
        row_copies.append(remote(src, part(b, 6 - n, 6, *lead), *sems, down, px))
        sent += count(src)
    await_rows(own_sem.at[0], own_rows)
    pl.semaphore_wait(barrier, len(near))
    for copy in row_copies:
        copy.start()

    strips = Strips(levels, cols)
    head, tail = strips.head, strips.tail
    tiles = [slice(r * SUB, (r + 1) * SUB) for r in range(nr + 1)]

    def pack_cols(items, tile):
        for rs in tiles[:nr]:
            ra = la = jnp.zeros((SUB, LANE), F32)
            for s, f in items:
                m = jnp.where(lane < LANE // 2, f(rs, head), f(rs, tail))
                m = roll(m, s, 1)
                ra = jnp.where((lane == s) | (lane == s + 1), m, ra)
                la = jnp.where(lane == (s + LANE - 1) % LANE, m, la)
            cs = slice(tile * LANE, (tile + 1) * LANE)
            p_right[rs, cs] = ra
            p_left[rs, cs] = la

    await_rows(in_sem.at[0], sum(count(b) for b in bufs[4:]))
    own_geo = geo_views(bufs[4:8])
    pack_cols([(2 * k, f) for k, f in enumerate(own_geo)], 1)
    await_rows(in_sem.at[1], sum(count(b) for b in bufs[:4]))
    items = []
    for l in range(levels):
        items += [(l * GROUP + 2 * k, f) for k, f in enumerate(level_views(l, bufs[:4]))]
    pack_cols(items, 0)

    def column(src, dst, i, y, x):
        return remote(src, dst, send_col.at[i], recv_col.at[i], y, x)

    col_copies = [
        column(p_right, g_right.at[0:rows], 0, py, left),
        column(p_left, g_left.at[0:rows], 1, py, right),
        column(p_right.at[rows - 2 : rows], g_right.at[rows + 4 : rows + 6], 2, down, left),
        column(p_right.at[0:2], g_right.at[rows + 2 : rows + 4], 3, up, left),
        column(p_left.at[0:2], g_left.at[rows + 2 : rows + 4], 4, up, right),
    ]
    for copy in col_copies:
        copy.start()

    for r in range(nr):
        for c in range(nc):
            put_geo(geo, span(r, c), [f(*span(r, c)) for f in own_geo], b_area[span(r, c)])

    for rs in tiles[:nr]:
        for k, x in enumerate(strips.own_levels(bufs[:4], rs)):
            slev[k, rs] = x
        for k, f in enumerate(own_geo + [view(b_area)]):
            sgeo[k, rs] = strips.own(f, rs)

    outputs_of = planes(o_vert, o_kin, o_cell, o_edge)

    def block(l):
        cc, dd, outs, _ = run(
            (nr, nc),
            fields((nr, nc), level_views(l, bufs[:4])),
            own_geo[6:12],
            own_geo[0:3],
            [view(geo, k) for k in range(9)],
        )
        for c in range(nc):
            for i, f in enumerate((cc, dd)):
                saved[i, l, :, span(0, c)[1]] = jnp.where(
                    sub < 4, roll(f(nr - 1, c), 2, 0), roll(f(0, c), -2, 0)
                )
        for r in range(nr):
            for c in range(nc):
                for (ref, lead), f in zip(outputs_of, outs):
                    ref[lead + (l,) + span(r, c)] = f(r, c)

    def inner(i, carry):
        for u in range(PAIR):
            block(i * PAIR + u)
        return carry

    lax.fori_loop(0, levels // PAIR, inner, 0)

    for copy in col_copies[:2]:
        copy.wait()
    grid = (nr, 1)
    last = slice(LANE, 2 * LANE)
    x = [
        Field(
            grid,
            lambda r, c, k=k: strips.with_level(
                k, slev[k, tiles[r]], g_right[tiles[r], head], g_left[tiles[r], 0:LANE]
            ),
        )
        for k in range(8)
    ]
    raw = [
        Field(
            grid,
            lambda r, c, k=k: strips.with_geo(
                k, sgeo[k, tiles[r]], g_right[tiles[r], last], g_left[tiles[r], last]
            ),
        )
        for k in range(14)
    ]
    cc, dd, outs, stages = strip_chain(grid, x, raw, lambda r, c: sgeo[14, tiles[r]])
    for stage in [x + raw] + stages + [outs]:
        build(stage)
    for i, f in enumerate((cc, dd)):
        ssaved[i] = jnp.where(sub < 4, roll(f(nr - 1, 0), 2, 0), roll(f(0, 0), -2, 0))
    for l in range(levels):
        for r in range(nr):
            moved = [pick(f(r, 0), strips.back[l]) for f in outs]
            for (ref, lead), z, (mf, me) in zip(outputs_of, moved, strips.masks()):
                if mf is not None:
                    pltpu.store(ref.at[lead + (l, tiles[r], head)], z, mask=mf)
                if me is not None:
                    pltpu.store(ref.at[lead + (l, tiles[r], tail)], z, mask=me)

    for copy in col_copies[2:]:
        copy.wait()
    await_rows(send_row.at[0], sent)
    await_rows(recv_row.at[0], sent)


def finish_kernel(*refs):
    kept = refs[0:4]
    bands = refs[4:13]
    g_right, g_left, saved, ssaved = refs[13:17]
    final = refs[17:21]
    ends = refs[21:25]
    kgeo, sem = refs[25:27]
    levels, rows, cols = kept[1].shape
    nr, nc = rows // SUB, cols // LANE
    sub, lane = iotas()
    copies = []

    def send(src, dst):
        copies.append(pltpu.make_async_copy(src, dst, sem.at[len(copies)]))
        copies[-1].start()

    def part(ref, a, b, *lead):
        rest = (slice(None),) * (len(ref.shape) - 2 - len(lead))
        return ref.at[lead + rest + (slice(a, b), slice(None))]

    if nr > 2:
        for a, b in zip(kept, final):
            send(part(a, SUB, rows - SUB), part(b, SUB, rows - SUB))

    strips = Strips(levels, cols)
    low, top = slice(0, SUB), slice(rows, rows + SUB)
    last, head = slice(LANE, 2 * LANE), slice(0, LANE)
    first_rows, last_rows = slice(0, SUB), slice(rows - SUB, rows)

    def border(g, cs):
        a, b = roll(g[last_rows, cs], 2, 0), roll(g[first_rows, cs], -2, 0)
        return jnp.where(sub < 2, a, jnp.where(sub >= 6, b, g[top, cs]))

    band_geo = geo_views(bands[4:8])
    one = (1, 1)
    const = lambda t: Field(one, lambda r, c: t)
    sides = [(border(g_right, cs), border(g_left, cs)) for cs in (head, last)]
    own_levels = strips.own_levels(bands[:4], low)
    own_geo = [strips.own(f, low) for f in band_geo]
    area = strips.own(view(bands[8]), low)
    x = [const(strips.with_level(k, own_levels[k], *sides[0])) for k in range(8)]
    raw = [const(strips.with_geo(k, own_geo[k], *sides[1])) for k in range(14)]
    for c in range(nc):
        at = span(0, c)
        put_geo(kgeo, at, [f(*at) for f in band_geo], bands[8][at])

    merge = (sub == 0) | (sub == SUB - 1)

    def swap_with(grid, load):
        return lambda i, f: Field(grid, lambda r, c: jnp.where(merge, load(i, c), f(r, c)))

    _, _, souts, sstages = strip_chain(
        one, x, raw, lambda r, c: area, swap_with(one, lambda i, c: ssaved[i])
    )
    grid = (1, nc)
    jobs = []
    for l in range(levels):
        jobs.append(
            run(
                grid,
                fields(grid, level_views(l, bands[:4])),
                band_geo[6:12],
                band_geo[0:3],
                [view(kgeo, k) for k in range(9)],
                swap_with(grid, lambda i, c, l=l: saved[i, l, :, span(0, c)[1]]),
            )[2:]
        )

    changed = [(0, 1), (1, 0), (1, 1), (1, 1), (1, 2), (1, 1), (2, 1)]
    src_of, end_of, dst_of = planes(*kept), planes(*ends), planes(*final)
    masks = strips.masks()

    def finalize(i):
        ref, lead = src_of[i]
        end = end_of[i][0]
        n_top, n_low = changed[i]
        y = souts[i](0, 0)
        zs = [pick(y, strips.back[l]) for l in range(levels)]
        for l in range(levels):
            for c in range(nc):
                cs = span(0, c)[1]
                t = jobs[l][0][i](0, c)
                for m, at in zip(masks[i], (0, nc - 1)):
                    if m is not None and at == c:
                        t = jnp.where(m, zs[l], t)
                for n, to, own, shift, where in (
                    (n_top, first_rows, first_rows, 2, sub < n_top),
                    (n_low, slice(SUB, 2 * SUB), last_rows, -2, sub >= SUB - n_low),
                ):
                    u = ref[lead + (l, own, cs)]
                    if n:
                        u = jnp.where(where, roll(t, shift, 0), u)
                    end[lead + (l, to, cs)] = u
        dst = dst_of[i][0]
        send(part(end, 0, SUB, *lead), part(dst, 0, SUB, *lead))
        send(part(end, SUB, 2 * SUB, *lead), part(dst, rows - SUB, rows, *lead))

    ready = [(), (0, 1, 2), (3,), (4, 5, 6)]
    for stage, done in enumerate(ready):
        for _, stages in jobs:
            build(stages[stage])
        build(sstages[stage])
        for i in done:
            finalize(i)
    for copy in copies:
        copy.wait()


def local(counts, vel, th, vt, tt, cd, el, area, kite, cor):
    args = (vel, th, vt, tt, cd, el, kite, cor, area)
    levels, rows, cols = th.shape
    outs = [(2, levels, rows, cols), (levels, rows, cols), (levels, rows, cols), (3, levels, rows, cols)]
    short = lambda s, n: s[:-2] + (n, cols)
    hbm, vmem = pl.BlockSpec(memory_space=pl.ANY), pl.BlockSpec(memory_space=pltpu.VMEM)
    side = (rows + SUB, 2 * LANE)
    passed = outs + [short(a.shape, SUB) for a in args]
    passed += [side, side, (2, levels, SUB, cols), (2, SUB, LANE)]
    kept = pl.pallas_call(
        lambda *refs: main_kernel(counts, *refs),
        out_shape=[pltpu.VMEM(s, F32) for s in passed],
        in_specs=[hbm] * len(args),
        out_specs=[vmem] * len(passed),
        scratch_shapes=[pltpu.VMEM(a.shape, F32) for a in args]
        + [
            pltpu.VMEM((rows, 2 * LANE), F32),
            pltpu.VMEM((rows, 2 * LANE), F32),
            pltpu.VMEM((9, rows, cols), F32),
            pltpu.VMEM((8, rows, LANE), F32),
            pltpu.VMEM((15, rows, LANE), F32),
            pltpu.VMEM((8 * levels * rows, 1, cols), F32),
        ]
        + [pltpu.SemaphoreType.DMA((n,)) for n in (2, 1, 1, 1, 5, 5)],
        compiler_params=pltpu.CompilerParams(collective_id=0, has_side_effects=True),
        name="main",
    )(*args)
    return pl.pallas_call(
        finish_kernel,
        out_shape=[jax.ShapeDtypeStruct(s, F32) for s in outs],
        in_specs=[vmem] * len(passed),
        out_specs=[pl.BlockSpec(memory_space=pltpu.HBM)] * len(outs),
        scratch_shapes=[pltpu.VMEM(short(s, 2 * SUB), F32) for s in outs]
        + [pltpu.VMEM((9, SUB, cols), F32), pltpu.SemaphoreType.DMA((18,))],
        name="finish",
    )(*[pltpu.with_memory_space_constraint(x, pltpu.VMEM) for x in kept])


def solution(mesh):
    counts = (mesh.shape["py"], mesh.shape["px"])
    p4, p3 = P(None, None, "py", "px"), P(None, "py", "px")
    return jax.shard_map(
        lambda *args: local(counts, *args),
        mesh=mesh,
        in_specs=(p4, p3, p4, p3, p3, p3, P("py", "px"), p4, p3),
        out_specs=(p4, p3, p3, p4),
        check_vma=False,
    )
```

time: 14.7 us -> 13.9 us (0.946)
  Pallas kernels: 13.9 us -> 13.1 us
    pallas_call x1, Pallas kernels: 12.7 us -> 11.1 us  [local(): pl.pallas_call(lambda *refs: main_kernel(counts, *refs), out_shape=[pltpu...]
    pallas_call x1, Pallas kernels: 1.26 us -> 2 us  [local(): pl.pallas_call(finish_kernel, out_shape=[jax.ShapeDtypeStruct(s, F32) for...]
where the time goes in v4:
time: 13.9 us; the launch traced here: 13.8 us
  Pallas kernels  13.1 us (94%)
  between operations  0.64 us (5%)
    pallas_call x1, Pallas kernels, local(): pl.pallas_call(lambda *refs: main_kernel(counts, *refs), out_shape=[pltpu...  11.1 us
    pallas_call x1, Pallas kernels, local(): pl.pallas_call(finish_kernel, out_shape=[jax.ShapeDtypeStruct(s, F32) for...  2 us

profile of v4, /device:TPU:0, one launch (start us, length us, event | category | flops | bytes accessed | tf_op | source)
XLA Modules:
  0.0 13.8 jit_solution(1890637806691292334)
XLA Ops:
  0.6 11.1 %main.1 = (f32[2,8,32,256]{3,2,1,0:T(8,128)S(1)}, f32[8,32,256]{2,1,0:T(8,128)S(1)}, f32[8,32,256]{2,1,0:T(8,128)S(1)}, f32[3,8,32,256]{3,2,1,0:T(8,128)S(1)}, f...) custom-call(f32[3,8,32,256]{3,2,1,0:T(8,128)} %refs_0_.1, ...), custom_call_target="tpu_custom_call" | custom-call | tf_op jit(solution)/shard_map/main/pallas_call | solution.py:581
  11.8 2.0 %finish.1 = (f32[2,8,32,256]{3,2,1,0:T(8,128)}, f32[8,32,256]{2,1,0:T(8,128)}, f32[8,32,256]{2,1,0:T(8,128)}, f32[3,8,32,256]{3,2,1,0:T(8,128)}) custom-call(f32[2,8,32,256]{3,2,1,0:T(8,128)S(1)} %get-tuple-element.21.refs_0_, f32[8,32,256]{2,1,0:T(8,128)S(1)} %get-tuple-element.22.refs_1_, f32[8,32,256]{2,1,0:T(8,128)S(1)} %get-tuple-element.23.refs_2_, ...), custom_call_target="tpu_custom_call" | custom-call | tf_op jit(solution)/shard_map/finish/pallas_call | solution.py:599

commit v5 on v4

--- a/solution.py
+++ b/solution.py
@@ -9,6 +9,8 @@
 LANE = 128
 GROUP = 16
 PAIR = 2
+SLOT = (0, 8, 9, 2, 4, 10, 11, 6)
+TWO = (0, 3, 4, 7)
 MESH = pl.DeviceIdType.MESH
 F32 = jnp.float32
 SLOPE = -0.5 / 36.0
@@ -171,6 +173,10 @@
     )
 
 
+def geo_slot(k):
+    return 12 if k == 0 else (1 + (k - 1) % 7) * GROUP + 12 + (k - 1) // 7
+
+
 def put_geo(dst, at, f, area):
     for k in range(3):
         dst[(k,) + at] = 0.25 * f[k] * f[3 + k]
@@ -228,11 +234,12 @@
         return jnp.where((pos == 11) | (pos == 12), right, jnp.where(pos == 1, left, x))
 
     def with_level(self, k, x, right, left):
-        return self.insert(x, roll(right, 11 - 2 * k, 1), roll(left, 2 - 2 * k, 1))
+        return self.insert(x, roll(right, 11 - SLOT[k], 1), roll(left, 2 - SLOT[k], 1))
 
     def with_geo(self, k, x, right, left):
-        rt = pick(right, jnp.where(self.pos == 12, 2 * k + 1, 2 * k))
-        lt = pick(left, jnp.full((SUB, LANE), (2 * k - 1) % LANE, jnp.int32))
+        at = geo_slot(k)
+        rt = pick(right, jnp.where(self.pos == 12, at + 1, at))
+        lt = pick(left, jnp.full((SUB, LANE), at - 1, jnp.int32))
         return self.insert(x, rt, lt)
 
     def masks(self):
@@ -348,26 +355,22 @@
     head, tail = strips.head, strips.tail
     tiles = [slice(r * SUB, (r + 1) * SUB) for r in range(nr + 1)]
 
-    def pack_cols(items, tile):
-        for rs in tiles[:nr]:
-            ra = la = jnp.zeros((SUB, LANE), F32)
-            for s, f in items:
-                m = jnp.where(lane < LANE // 2, f(rs, head), f(rs, tail))
-                m = roll(m, s, 1)
-                ra = jnp.where((lane == s) | (lane == s + 1), m, ra)
-                la = jnp.where(lane == (s + LANE - 1) % LANE, m, la)
-            cs = slice(tile * LANE, (tile + 1) * LANE)
-            p_right[rs, cs] = ra
-            p_left[rs, cs] = la
-
     await_rows(in_sem.at[0], sum(count(b) for b in bufs[4:]))
     own_geo = geo_views(bufs[4:8])
-    pack_cols([(2 * k, f) for k, f in enumerate(own_geo)], 1)
+    items = [(geo_slot(k), k == 0, f) for k, f in enumerate(own_geo)]
+    for l in range(levels):
+        for k, f in enumerate(level_views(l, bufs[:4])):
+            items.append((l * GROUP + SLOT[k], k in TWO, f))
     await_rows(in_sem.at[1], sum(count(b) for b in bufs[:4]))
-    items = []
-    for l in range(levels):
-        items += [(l * GROUP + 2 * k, f) for k, f in enumerate(level_views(l, bufs[:4]))]
-    pack_cols(items, 0)
+    for rs in tiles[:nr]:
+        ra = la = jnp.zeros((SUB, LANE), F32)
+        for s, two, f in items:
+            m = jnp.where(lane < LANE // 2, f(rs, head), f(rs, tail))
+            m = roll(m, s, 1)
+            ra = jnp.where((lane == s) | (lane == s + 1) if two else lane == s, m, ra)
+            la = jnp.where(lane == (s + LANE - 1) % LANE, m, la)
+        p_right[rs] = ra
+        p_left[rs] = la
 
     def column(src, dst, i, y, x):
         return remote(src, dst, send_col.at[i], recv_col.at[i], y, x)
@@ -422,12 +425,11 @@
     for copy in col_copies[:2]:
         copy.wait()
     grid = (nr, 1)
-    last = slice(LANE, 2 * LANE)
     x = [
         Field(
             grid,
             lambda r, c, k=k: strips.with_level(
-                k, slev[k, tiles[r]], g_right[tiles[r], head], g_left[tiles[r], 0:LANE]
+                k, slev[k, tiles[r]], g_right[tiles[r]], g_left[tiles[r]]
             ),
         )
         for k in range(8)
@@ -436,7 +438,7 @@
         Field(
             grid,
             lambda r, c, k=k: strips.with_geo(
-                k, sgeo[k, tiles[r]], g_right[tiles[r], last], g_left[tiles[r], last]
+                k, sgeo[k, tiles[r]], g_right[tiles[r]], g_left[tiles[r]]
             ),
         )
         for k in range(14)
@@ -471,38 +473,41 @@
     levels, rows, cols = kept[1].shape
     nr, nc = rows // SUB, cols // LANE
     sub, lane = iotas()
-    copies = []
-
-    def send(src, dst):
-        copies.append(pltpu.make_async_copy(src, dst, sem.at[len(copies)]))
-        copies[-1].start()
+
+    def send(src, dst, which):
+        pltpu.make_async_copy(src, dst, sem.at[which]).start()
 
     def part(ref, a, b, *lead):
         rest = (slice(None),) * (len(ref.shape) - 2 - len(lead))
         return ref.at[lead + rest + (slice(a, b), slice(None))]
 
+    changed = [(0, 1), (1, 0), (1, 1), (1, 1), (1, 2), (1, 1), (2, 1)]
+    array_of = (0, 0, 1, 2, 3, 3, 3)
+    src_of, end_of, dst_of = planes(*kept), planes(*ends), planes(*final)
     if nr > 2:
-        for a, b in zip(kept, final):
-            send(part(a, SUB, rows - SUB), part(b, SUB, rows - SUB))
+        for i, (a, b) in enumerate(zip(kept, final)):
+            send(part(a, SUB, rows - SUB), part(b, SUB, rows - SUB), i)
+    for (src, lead), (dst, _), (n_top, n_low), which in zip(src_of, dst_of, changed, array_of):
+        for a, b in ((n_top, SUB), (rows - SUB, rows - n_low)):
+            send(part(src, a, b, *lead), part(dst, a, b, *lead), which)
 
     strips = Strips(levels, cols)
     low, top = slice(0, SUB), slice(rows, rows + SUB)
-    last, head = slice(LANE, 2 * LANE), slice(0, LANE)
     first_rows, last_rows = slice(0, SUB), slice(rows - SUB, rows)
 
-    def border(g, cs):
-        a, b = roll(g[last_rows, cs], 2, 0), roll(g[first_rows, cs], -2, 0)
-        return jnp.where(sub < 2, a, jnp.where(sub >= 6, b, g[top, cs]))
+    def border(g):
+        a, b = roll(g[last_rows], 2, 0), roll(g[first_rows], -2, 0)
+        return jnp.where(sub < 2, a, jnp.where(sub >= 6, b, g[top]))
 
     band_geo = geo_views(bands[4:8])
     one = (1, 1)
     const = lambda t: Field(one, lambda r, c: t)
-    sides = [(border(g_right, cs), border(g_left, cs)) for cs in (head, last)]
+    sides = border(g_right), border(g_left)
     own_levels = strips.own_levels(bands[:4], low)
     own_geo = [strips.own(f, low) for f in band_geo]
     area = strips.own(view(bands[8]), low)
-    x = [const(strips.with_level(k, own_levels[k], *sides[0])) for k in range(8)]
-    raw = [const(strips.with_geo(k, own_geo[k], *sides[1])) for k in range(14)]
+    x = [const(strips.with_level(k, own_levels[k], *sides)) for k in range(8)]
+    raw = [const(strips.with_geo(k, own_geo[k], *sides)) for k in range(14)]
     for c in range(nc):
         at = span(0, c)
         put_geo(kgeo, at, [f(*at) for f in band_geo], bands[8][at])
@@ -529,34 +534,25 @@
             )[2:]
         )
 
-    changed = [(0, 1), (1, 0), (1, 1), (1, 1), (1, 2), (1, 1), (2, 1)]
-    src_of, end_of, dst_of = planes(*kept), planes(*ends), planes(*final)
     masks = strips.masks()
 
     def finalize(i):
-        ref, lead = src_of[i]
-        end = end_of[i][0]
+        end, lead = end_of[i]
+        dst = dst_of[i][0]
         n_top, n_low = changed[i]
         y = souts[i](0, 0)
         zs = [pick(y, strips.back[l]) for l in range(levels)]
         for l in range(levels):
             for c in range(nc):
-                cs = span(0, c)[1]
                 t = jobs[l][0][i](0, c)
                 for m, at in zip(masks[i], (0, nc - 1)):
                     if m is not None and at == c:
                         t = jnp.where(m, zs[l], t)
-                for n, to, own, shift, where in (
-                    (n_top, first_rows, first_rows, 2, sub < n_top),
-                    (n_low, slice(SUB, 2 * SUB), last_rows, -2, sub >= SUB - n_low),
-                ):
-                    u = ref[lead + (l, own, cs)]
-                    if n:
-                        u = jnp.where(where, roll(t, shift, 0), u)
-                    end[lead + (l, to, cs)] = u
-        dst = dst_of[i][0]
-        send(part(end, 0, SUB, *lead), part(dst, 0, SUB, *lead))
-        send(part(end, SUB, 2 * SUB, *lead), part(dst, rows - SUB, rows, *lead))
+                end[lead + (l,) + span(0, c)] = t
+        if n_top:
+            send(part(end, 6, 6 + n_top, *lead), part(dst, 0, n_top, *lead), array_of[i])
+        if n_low:
+            send(part(end, 2 - n_low, 2, *lead), part(dst, rows - n_low, rows, *lead), array_of[i])
 
     ready = [(), (0, 1, 2), (3,), (4, 5, 6)]
     for stage, done in enumerate(ready):
@@ -565,8 +561,8 @@
         build(sstages[stage])
         for i in done:
             finalize(i)
-    for copy in copies:
-        copy.wait()
+    for i, (a, b) in enumerate(zip(kept, final)):
+        pltpu.make_async_copy(a, b, sem.at[i]).wait()
 
 
 def local(counts, vel, th, vt, tt, cd, el, area, kite, cor):
@@ -575,7 +571,7 @@
     outs = [(2, levels, rows, cols), (levels, rows, cols), (levels, rows, cols), (3, levels, rows, cols)]
     short = lambda s, n: s[:-2] + (n, cols)
     hbm, vmem = pl.BlockSpec(memory_space=pl.ANY), pl.BlockSpec(memory_space=pltpu.VMEM)
-    side = (rows + SUB, 2 * LANE)
+    side = (rows + SUB, LANE)
     passed = outs + [short(a.shape, SUB) for a in args]
     passed += [side, side, (2, levels, SUB, cols), (2, SUB, LANE)]
     kept = pl.pallas_call(
@@ -585,8 +581,8 @@
         out_specs=[vmem] * len(passed),
         scratch_shapes=[pltpu.VMEM(a.shape, F32) for a in args]
         + [
-            pltpu.VMEM((rows, 2 * LANE), F32),
-            pltpu.VMEM((rows, 2 * LANE), F32),
+            pltpu.VMEM((rows, LANE), F32),
+            pltpu.VMEM((rows, LANE), F32),
             pltpu.VMEM((9, rows, cols), F32),
             pltpu.VMEM((8, rows, LANE), F32),
             pltpu.VMEM((15, rows, LANE), F32),
@@ -601,8 +597,8 @@
         out_shape=[jax.ShapeDtypeStruct(s, F32) for s in outs],
         in_specs=[vmem] * len(passed),
         out_specs=[pl.BlockSpec(memory_space=pltpu.HBM)] * len(outs),
-        scratch_shapes=[pltpu.VMEM(short(s, 2 * SUB), F32) for s in outs]
-        + [pltpu.VMEM((9, SUB, cols), F32), pltpu.SemaphoreType.DMA((18,))],
+        scratch_shapes=[pltpu.VMEM(short(s, SUB), F32) for s in outs]
+        + [pltpu.VMEM((9, SUB, cols), F32), pltpu.SemaphoreType.DMA((4,))],
         name="finish",
     )(*[pltpu.with_memory_space_constraint(x, pltpu.VMEM) for x in kept])
 

time: 13.9 us -> 13.4 us (0.964)
  Pallas kernels: 13.1 us -> 12.6 us
    pallas_call x1, Pallas kernels: 2 us -> 1.5 us  [local(): pl.pallas_call(finish_kernel, out_shape=[jax.ShapeDtypeStruct(s, F32) for...]
where the time goes in v5:
time: 13.4 us; the launch traced here: 13.3 us
  Pallas kernels  12.6 us (94%)
  between operations  0.64 us (5%)
    pallas_call x1, Pallas kernels, local(): pl.pallas_call(lambda *refs: main_kernel(counts, *refs), out_shape=[pltpu...  11.1 us
    pallas_call x1, Pallas kernels, local(): pl.pallas_call(finish_kernel, out_shape=[jax.ShapeDtypeStruct(s, F32) for...  1.5 us

profile of v5, /device:TPU:0, one launch (start us, length us, event | category | flops | bytes accessed | tf_op | source)
XLA Modules:
  0.0 13.3 jit_solution(5765870770352652099)
XLA Ops:
  0.6 11.1 %main.1 = (f32[2,8,32,256]{3,2,1,0:T(8,128)S(1)}, f32[8,32,256]{2,1,0:T(8,128)S(1)}, f32[8,32,256]{2,1,0:T(8,128)S(1)}, f32[3,8,32,256]{3,2,1,0:T(8,128)S(1)}, f...) custom-call(f32[3,8,32,256]{3,2,1,0:T(8,128)} %refs_0_.1, ...), custom_call_target="tpu_custom_call" | custom-call | tf_op jit(solution)/shard_map/main/pallas_call | solution.py:577
  11.8 1.5 %finish.1 = (f32[2,8,32,256]{3,2,1,0:T(8,128)}, f32[8,32,256]{2,1,0:T(8,128)}, f32[8,32,256]{2,1,0:T(8,128)}, f32[3,8,32,256]{3,2,1,0:T(8,128)}) custom-call(f32[2,8,32,256]{3,2,1,0:T(8,128)S(1)} %get-tuple-element.21.refs_0_, f32[8,32,256]{2,1,0:T(8,128)S(1)} %get-tuple-element.22.refs_1_, f32[8,32,256]{2,1,0:T(8,128)S(1)} %get-tuple-element.23.refs_2_, ...), custom_call_target="tpu_custom_call" | custom-call | tf_op jit(solution)/shard_map/finish/pallas_call | solution.py:595

commit v6 on v5

--- a/solution.py
+++ b/solution.py
@@ -9,6 +9,7 @@
 LANE = 128
 GROUP = 16
 PAIR = 2
+PARTS = 2
 SLOT = (0, 8, 9, 2, 4, 10, 11, 6)
 TWO = (0, 3, 4, 7)
 MESH = pl.DeviceIdType.MESH
@@ -306,16 +307,18 @@
             n *= d
         return n
 
-    own = []
     for a, b in zip(hbm, bands):
-        own.append(pltpu.make_async_copy(part(a, rows - 2, rows), part(b, 0, 2), own_sem.at[0]))
-        own.append(pltpu.make_async_copy(part(a, 0, 2), part(b, 6, 8), own_sem.at[0]))
-    for copy in own:
-        copy.start()
-    own_rows = sum(4 * count(b) // SUB for b in bands)
-    late = (4, 5, 6, 7, 8, 0, 1, 2, 3)
-    for i in late:
-        pltpu.make_async_copy(hbm[i], bufs[i], in_sem.at[0 if i >= 4 else 1]).start()
+        pltpu.make_async_copy(part(a, rows - 2, rows), part(b, 0, 2), own_sem.at[0]).start()
+    for a, b in zip(hbm, bands):
+        pltpu.make_async_copy(part(a, 0, 2), part(b, 6, 8), own_sem.at[1]).start()
+    own_rows = sum(2 * count(b) // SUB for b in bands)
+    for i in (4, 5, 6, 7, 8):
+        pltpu.make_async_copy(hbm[i], bufs[i], in_sem.at[0]).start()
+    cuts = [slice(i * levels // PARTS, (i + 1) * levels // PARTS) for i in range(PARTS)]
+    for j, cut in enumerate(cuts):
+        for a, b in zip(hbm[:4], bufs):
+            at = (slice(None),) * (len(a.shape) - 3) + (cut,)
+            pltpu.make_async_copy(a.at[at], b.at[at], in_sem.at[1 + j]).start()
 
     def remote(src, dst, send, recv, y, x):
         return pltpu.make_async_remote_copy(
@@ -337,18 +340,18 @@
         (2, cd, slice(0, 2)), (1, cd, 2), (1, el, 0), (2, kite, 0), (1, kite, 1), (2, cor, 0), (1, cor, 1),
     ]
     sems = (send_row.at[0], recv_row.at[0])
-    row_copies, sent = [], 0
+    up_copies, down_copies, sent = [], [], 0
     for n, b, *lead in to_up:
         src = part(b, 6, 6 + n, *lead)
-        row_copies.append(remote(src, part(b, 2, 2 + n, *lead), *sems, up, px))
+        up_copies.append(remote(src, part(b, 2, 2 + n, *lead), *sems, up, px))
         sent += count(src)
     for n, b, *lead in to_down:
         src = part(b, 2 - n, 2, *lead)
-        row_copies.append(remote(src, part(b, 6 - n, 6, *lead), *sems, down, px))
+        down_copies.append(remote(src, part(b, 6 - n, 6, *lead), *sems, down, px))
         sent += count(src)
     await_rows(own_sem.at[0], own_rows)
     pl.semaphore_wait(barrier, len(near))
-    for copy in row_copies:
+    for copy in down_copies:
         copy.start()
 
     strips = Strips(levels, cols)
@@ -357,20 +360,28 @@
 
     await_rows(in_sem.at[0], sum(count(b) for b in bufs[4:]))
     own_geo = geo_views(bufs[4:8])
-    items = [(geo_slot(k), k == 0, f) for k, f in enumerate(own_geo)]
-    for l in range(levels):
-        for k, f in enumerate(level_views(l, bufs[:4])):
-            items.append((l * GROUP + SLOT[k], k in TWO, f))
-    await_rows(in_sem.at[1], sum(count(b) for b in bufs[:4]))
-    for rs in tiles[:nr]:
-        ra = la = jnp.zeros((SUB, LANE), F32)
-        for s, two, f in items:
-            m = jnp.where(lane < LANE // 2, f(rs, head), f(rs, tail))
-            m = roll(m, s, 1)
-            ra = jnp.where((lane == s) | (lane == s + 1) if two else lane == s, m, ra)
-            la = jnp.where(lane == (s + LANE - 1) % LANE, m, la)
-        p_right[rs] = ra
-        p_left[rs] = la
+    packed = [[jnp.zeros((SUB, LANE), F32)] * 2 for _ in range(nr)]
+
+    def pack(items):
+        for r in range(nr):
+            rs, (ra, la) = tiles[r], packed[r]
+            for s, two, f in items:
+                m = jnp.where(lane < LANE // 2, f(rs, head), f(rs, tail))
+                m = roll(m, s, 1)
+                ra = jnp.where((lane == s) | (lane == s + 1) if two else lane == s, m, ra)
+                la = jnp.where(lane == (s + LANE - 1) % LANE, m, la)
+            packed[r] = [ra, la]
+
+    pack([(geo_slot(k), k == 0, f) for k, f in enumerate(own_geo)])
+    for j, cut in enumerate(cuts):
+        await_rows(in_sem.at[1 + j], sum(count(b) for b in bufs[:4]) // PARTS)
+        items = []
+        for l in range(cut.start, cut.stop):
+            for k, f in enumerate(level_views(l, bufs[:4])):
+                items.append((l * GROUP + SLOT[k], k in TWO, f))
+        pack(items)
+    for r in range(nr):
+        p_right[tiles[r]], p_left[tiles[r]] = packed[r]
 
     def column(src, dst, i, y, x):
         return remote(src, dst, send_col.at[i], recv_col.at[i], y, x)
@@ -383,6 +394,9 @@
         column(p_left.at[0:2], g_left.at[rows + 2 : rows + 4], 4, up, right),
     ]
     for copy in col_copies:
+        copy.start()
+    await_rows(own_sem.at[1], own_rows)
+    for copy in up_copies:
         copy.start()
 
     for r in range(nr):
@@ -588,7 +602,7 @@
             pltpu.VMEM((15, rows, LANE), F32),
             pltpu.VMEM((8 * levels * rows, 1, cols), F32),
         ]
-        + [pltpu.SemaphoreType.DMA((n,)) for n in (2, 1, 1, 1, 5, 5)],
+        + [pltpu.SemaphoreType.DMA((n,)) for n in (1 + PARTS, 2, 1, 1, 5, 5)],
         compiler_params=pltpu.CompilerParams(collective_id=0, has_side_effects=True),
         name="main",
     )(*args)

time: 13.4 us -> 12.8 us (0.955)
  Pallas kernels: 12.6 us -> 12 us
    pallas_call x1, Pallas kernels: 11.1 us -> 10.5 us  [local(): pl.pallas_call(lambda *refs: main_kernel(counts, *refs), out_shape=[pltpu...]
where the time goes in v6:
time: 12.8 us; the launch traced here: 12.7 us
  Pallas kernels  12 us (94%)
  between operations  0.64 us (5%)
    pallas_call x1, Pallas kernels, local(): pl.pallas_call(lambda *refs: main_kernel(counts, *refs), out_shape=[pltpu...  10.5 us
    pallas_call x1, Pallas kernels, local(): pl.pallas_call(finish_kernel, out_shape=[jax.ShapeDtypeStruct(s, F32) for...  1.5 us

profile of v6, /device:TPU:0, one launch (start us, length us, event | category | flops | bytes accessed | tf_op | source)
XLA Modules:
  0.0 12.7 jit_solution(4731951460558886426)
XLA Ops:
  0.6 10.5 %main.1 = (f32[2,8,32,256]{3,2,1,0:T(8,128)S(1)}, f32[8,32,256]{2,1,0:T(8,128)S(1)}, f32[8,32,256]{2,1,0:T(8,128)S(1)}, f32[3,8,32,256]{3,2,1,0:T(8,128)S(1)}, f...) custom-call(f32[3,8,32,256]{3,2,1,0:T(8,128)} %refs_0_.1, ...), custom_call_target="tpu_custom_call" | custom-call | tf_op jit(solution)/shard_map/main/pallas_call | solution.py:591
  11.2 1.5 %finish.1 = (f32[2,8,32,256]{3,2,1,0:T(8,128)}, f32[8,32,256]{2,1,0:T(8,128)}, f32[8,32,256]{2,1,0:T(8,128)}, f32[3,8,32,256]{3,2,1,0:T(8,128)}) custom-call(f32[2,8,32,256]{3,2,1,0:T(8,128)S(1)} %get-tuple-element.21.refs_0_, f32[8,32,256]{2,1,0:T(8,128)S(1)} %get-tuple-element.22.refs_1_, f32[8,32,256]{2,1,0:T(8,128)S(1)} %get-tuple-element.23.refs_2_, ...), custom_call_target="tpu_custom_call" | custom-call | tf_op jit(solution)/shard_map/finish/pallas_call | solution.py:609

commit v7 on v6

--- a/solution.py
+++ b/solution.py
@@ -239,9 +239,9 @@
 
     def with_geo(self, k, x, right, left):
         at = geo_slot(k)
-        rt = pick(right, jnp.where(self.pos == 12, at + 1, at))
-        lt = pick(left, jnp.full((SUB, LANE), at - 1, jnp.int32))
-        return self.insert(x, rt, lt)
+        m = jnp.where(self.lane == at - 1, left, right)
+        y = pick(m, jnp.where(self.pos == 11, at, jnp.where(self.pos == 12, at + 1, at - 1)))
+        return self.insert(x, y, y)
 
     def masks(self):
         lane = self.lane

time: 12.8 us -> 12.8 us (level)
  no operation moved by 1% of the time
where the time goes in v7:
time: 12.8 us; the launch traced here: 12.6 us
  Pallas kernels  12 us (94%)
  between operations  0.64 us (5%)
    pallas_call x1, Pallas kernels, local(): pl.pallas_call(lambda *refs: main_kernel(counts, *refs), out_shape=[pltpu...  10.5 us
    pallas_call x1, Pallas kernels, local(): pl.pallas_call(finish_kernel, out_shape=[jax.ShapeDtypeStruct(s, F32) for...  1.47 us

profile of v7, /device:TPU:0, one launch (start us, length us, event | category | flops | bytes accessed | tf_op | source)
XLA Modules:
  0.0 12.6 jit_solution(16111047770437240988)
XLA Ops:
  0.6 10.5 %main.1 = (f32[2,8,32,256]{3,2,1,0:T(8,128)S(1)}, f32[8,32,256]{2,1,0:T(8,128)S(1)}, f32[8,32,256]{2,1,0:T(8,128)S(1)}, f32[3,8,32,256]{3,2,1,0:T(8,128)S(1)}, f...) custom-call(f32[3,8,32,256]{3,2,1,0:T(8,128)} %refs_0_.1, ...), custom_call_target="tpu_custom_call" | custom-call | tf_op jit(solution)/shard_map/main/pallas_call | solution.py:591
  11.1 1.5 %finish.1 = (f32[2,8,32,256]{3,2,1,0:T(8,128)}, f32[8,32,256]{2,1,0:T(8,128)}, f32[8,32,256]{2,1,0:T(8,128)}, f32[3,8,32,256]{3,2,1,0:T(8,128)}) custom-call(f32[2,8,32,256]{3,2,1,0:T(8,128)S(1)} %get-tuple-element.21.refs_0_, f32[8,32,256]{2,1,0:T(8,128)S(1)} %get-tuple-element.22.refs_1_, f32[8,32,256]{2,1,0:T(8,128)S(1)} %get-tuple-element.23.refs_2_, ...), custom_call_target="tpu_custom_call" | custom-call | tf_op jit(solution)/shard_map/finish/pallas_call | solution.py:609

commit v8 on v7

--- a/solution.py
+++ b/solution.py
@@ -70,17 +70,18 @@
     def parts(vv, hh):
         flux = [lift(lambda a, b: a * b, vv[k], dist[k]) for k in range(3)]
         c0 = lift(lambda a, b, c: a + b - c, flux[0], row_shift(flux[2], 1), flux[1])
-        c1 = lift(lambda a, b, c: a - b - c, flux[1], flux[2], col_shift(row_shift(flux[0], -1), 1))
+        fc = col_shift(row_shift(flux[0], -1), 1)
+        c1 = lift(lambda a, b, c: a - b - c, flux[1], flux[2], fc)
         hc = col_shift(hh, 1)
         hr = row_shift(hh, 1)
         hd = row_shift(hc, -1)
         mix = lambda a, b, c, p, q, s: a * p + b * q + c * s
         h0 = lift(mix, kt[0], kt[1], kt[2], hh, hr, hc)
         h1 = lift(mix, kt[3], kt[4], kt[5], hh, hc, hd)
-        return (c0, c1), (h0, h1)
-
-    cv, hv = parts(v, h)
-    cw, hw = parts(t, g)
+        return (c0, c1), (h0, h1), [hc, fc]
+
+    cv, hv, moved_v = parts(v, h)
+    cw, hw, moved_t = parts(t, g)
 
     def potential(k):
         def make(r, c):
@@ -146,7 +147,7 @@
             lift(lambda a: a * (1.0 / 36.0), cc),
         ] + [edge(k) for k in range(3)]
 
-    stages = [[*cv, *hv, *cw, *hw, e_low], [p0, q0, p1, q1], [cc, dd, p1_low], [*cn, *dn]]
+    stages = [moved_v + moved_t, [p0, q0, p1, q1, e_low], [cc, dd, p1_low], [*cn, *dn]]
     return cc, dd, outputs, stages
 
 
@@ -395,14 +396,14 @@
     ]
     for copy in col_copies:
         copy.start()
+
+    for r in range(nr):
+        for c in range(nc):
+            put_geo(geo, span(r, c), [f(*span(r, c)) for f in own_geo], b_area[span(r, c)])
+
     await_rows(own_sem.at[1], own_rows)
     for copy in up_copies:
         copy.start()
-
-    for r in range(nr):
-        for c in range(nc):
-            put_geo(geo, span(r, c), [f(*span(r, c)) for f in own_geo], b_area[span(r, c)])
-
     for rs in tiles[:nr]:
         for k, x in enumerate(strips.own_levels(bufs[:4], rs)):
             slev[k, rs] = x

time: 12.8 us -> 12.7 us (level)
  no operation moved by 1% of the time
where the time goes in v8:
time: 12.7 us; the launch traced here: 12.6 us
  Pallas kernels  11.9 us (94%)
  between operations  0.64 us (5%)
    pallas_call x1, Pallas kernels, local(): pl.pallas_call(lambda *refs: main_kernel(counts, *refs), out_shape=[pltpu...  10.5 us
    pallas_call x1, Pallas kernels, local(): pl.pallas_call(finish_kernel, out_shape=[jax.ShapeDtypeStruct(s, F32) for...  1.45 us

profile of v8, /device:TPU:0, one launch (start us, length us, event | category | flops | bytes accessed | tf_op | source)
XLA Modules:
  0.0 12.6 jit_solution(5259130034554426053)
XLA Ops:
  0.6 10.5 %main.1 = (f32[2,8,32,256]{3,2,1,0:T(8,128)S(1)}, f32[8,32,256]{2,1,0:T(8,128)S(1)}, f32[8,32,256]{2,1,0:T(8,128)S(1)}, f32[3,8,32,256]{3,2,1,0:T(8,128)S(1)}, f...) custom-call(f32[3,8,32,256]{3,2,1,0:T(8,128)} %refs_0_.1, ...), custom_call_target="tpu_custom_call" | custom-call | tf_op jit(solution)/shard_map/main/pallas_call | solution.py:592
  11.1 1.5 %finish.1 = (f32[2,8,32,256]{3,2,1,0:T(8,128)}, f32[8,32,256]{2,1,0:T(8,128)}, f32[8,32,256]{2,1,0:T(8,128)}, f32[3,8,32,256]{3,2,1,0:T(8,128)}) custom-call(f32[2,8,32,256]{3,2,1,0:T(8,128)S(1)} %get-tuple-element.21.refs_0_, f32[8,32,256]{2,1,0:T(8,128)S(1)} %get-tuple-element.22.refs_1_, f32[8,32,256]{2,1,0:T(8,128)S(1)} %get-tuple-element.23.refs_2_, ...), custom_call_target="tpu_custom_call" | custom-call | tf_op jit(solution)/shard_map/finish/pallas_call | solution.py:610
